TPU v7x, 128 devices: a whole 4x4x4 slice. The times are simulated.
128 devices in a mesh: tp: 4 (over x), dp: 32 (over z, y, core).
Axes of the slice: x: 4, y: 4, z: 4, core: 2. Of those that a mesh axis runs over, the one named last changes fastest.
Arguments:
- hidden: bfloat16 [2048, 896], P('dp')
- norm_w: bfloat16 [896], replicated
- emb_table: bfloat16 [151936, 896], P('tp')
- teacher: bfloat16 [2048, 151936], P('dp', 'tp')
- loss_mask: int32 [2048], P('dp')
Outputs:
- output 1: float32 [], replicated
- output 2: bfloat16 [2048, 896], P('dp')
- output 3: float32 [151936, 896], P('tp', 'dp')
- output 4: float32 [896], replicated
All inputs are finite; a program needn't handle non-finite values.
Results may differ from a plain program's by a relative error of at most 0.001.
Values sent between devices are 32-bit elements.
A program may use at most 1 GiB of HBM per device.

v0:
```python
import jax
import jax.numpy as jnp
from jax import lax
from jax.sharding import PartitionSpec as P

SOFT_CAP = 30.0
NORM_EPS = 1e-6


def rms_norm(hid_f32, scale_f32):
    inv_rms = lax.rsqrt(jnp.mean(hid_f32 * hid_f32, axis=-1, keepdims=True) + NORM_EPS)
    return hid_f32 * inv_rms * (1.0 + scale_f32)


def solution(mesh):
    def device_fn(hid_loc, norm_w, emb_loc, teach_loc, mask_loc):
        mask_f32 = mask_loc.astype(jnp.float32)
        tok_count = lax.psum(jnp.sum(mask_f32), 'dp')
        weight = mask_f32 / tok_count
        normed_f32, norm_pull = jax.vjp(rms_norm, hid_loc.astype(jnp.float32), norm_w.astype(jnp.float32))
        normed = normed_f32.astype(jnp.bfloat16)
        raw_logit = jnp.einsum('nd,vd->nv', normed, emb_loc, preferred_element_type=jnp.float32)
        tanh_val = jnp.tanh(raw_logit / SOFT_CAP)
        capped = SOFT_CAP * tanh_val
        teach_f32 = teach_loc.astype(jnp.float32)
        maxima = lax.pmax(jnp.stack([jnp.max(capped, axis=-1), jnp.max(teach_f32, axis=-1)], axis=-1), 'tp')
        stu_exp = jnp.exp(capped - maxima[:, 0:1])
        tea_exp = jnp.exp(teach_f32 - maxima[:, 1:2])
        local_sums = jnp.stack([jnp.sum(stu_exp, axis=-1), jnp.sum(tea_exp, axis=-1), jnp.sum(tea_exp * (teach_f32 - capped), axis=-1)], axis=-1)
        totals = lax.psum(local_sums, 'tp')
        lse_stu = maxima[:, 0] + jnp.log(totals[:, 0])
        lse_tea = maxima[:, 1] + jnp.log(totals[:, 1])
        kl_tok = totals[:, 2] / totals[:, 1] - lse_tea + lse_stu
        loss_val = lax.psum(jnp.sum(weight * kl_tok), 'dp')
        prob_diff = stu_exp / totals[:, 0:1] - tea_exp / totals[:, 1:2]
        d_raw = (prob_diff * weight[:, None] * (1.0 - tanh_val * tanh_val)).astype(jnp.bfloat16)
        grad_normed = lax.psum(jnp.dot(d_raw, emb_loc, preferred_element_type=jnp.float32), 'tp')
        emb_part = jnp.einsum('nv,nd->vd', d_raw, normed, preferred_element_type=jnp.float32)
        grad_emb = lax.psum_scatter(emb_part, 'dp', scatter_dimension=1, tiled=True)
        grad_hid, grad_scale = norm_pull(grad_normed)
        grad_w = lax.psum(grad_scale, 'dp')
        return loss_val, grad_hid.astype(jnp.bfloat16), grad_emb, grad_w

    return jax.shard_map(device_fn, mesh=mesh, in_specs=(P('dp', None), P(None), P('tp', None), P('dp', 'tp'), P('dp')), out_specs=(P(), P('dp', None), P('tp', 'dp'), P(None)), check_vma=False)
```

profile of v0, /device:TPU:1, one launch (start us, length us, event | category | flops | bytes accessed | tf_op | source)
XLA Modules:
  0.0 1583.6 jit_solution(3929146693587679853)
XLA Ops:
  7.2 0.0 all-reduce.5.cloned.1.call-start
  7.2 0.7 convert_add_fusion
  7.9 1.0 fusion.17
  8.9 3.1 reduce_max.26
  12.1 0.0 copy-start.3
  12.1 31.2 %multiply_reduce_fusion = (f32[64]{0:T(128)S(1)}, f32[64,37984]{1,0:T(8,128)}) fusion(bf16[37984,896]{1,0:T(8,128)(2,1)} %param.7, bf16[64,896]{1,0:T(8,128)(2,1)} %param.5, f32[896]{0:T(1024)S(1)} %convert_add_fusion, f32[64]{0:T(128)S(1)} %fusion.23), kind=kOutput, calls=%fused_computation.15 | convolution fusion | flops 4363831296 | bytes 77910016 | tf_op jit(solution)/shard_map/nd,vd->nv/dot_general | solution.py:22
  43.3 0.0 copy-start
  43.3 9.3 pmax.7
  52.6 0.6 convert_reduce_fusion
  53.2 7.8 fusion.11
  61.0 6.0 psum.36
  67.0 68.6 %psum.35 = f32[]{:T(128)} all-reduce(f32[]{:T(128)} %convert_reduce_fusion), channel_id=1, replica_groups=mesh['tp'=4,'dp'=32] {'dp'}, use_global_device_ids=true, to_apply=%region_1.0 | all-reduce | flops 1 | bytes 8 | tf_op jit(solution)/shard_map/psum | solution.py:18
  135.7 1.3 multiply_reduce_fusion.1
  136.9 50.7 %fusion.19 = f32[37984,896]{0,1:T(8,128)} fusion(bf16[64,896]{1,0:T(8,128)(2,1)S(1)} %copy-done, f32[896]{0:T(1024)S(1)} %convert_add_fusion, f32[64]{0:T(128)S(1)} %fusion.23, f32[64,37984]{1,0:T(8,128)} %get-tuple-element.18, bf16[64,37984]{1,0:T(8,128)(2,1)} %param.8, f32[64]{0:T(128)S(1)} %get-tuple-element.12, f32[64]{0:T(128)S(1)} %get-tuple-element.14, ...), kind=kOutput, calls=%fused_computation.28 | convolution fusion | flops 4385710080 | bytes 150840320 | tf_op jit(solution)/shard_map/nv,nd->vd/dot_general | solution.py:38
  187.6 859.8 %fusion = f32[37984,32]{0,1:T(8,128)} fusion(f32[37984,896]{0,1:T(8,128)} %fusion.19), kind=kCustom, calls=%all-reduce-scatter | all-reduce-scatter fusion | flops 38895616 | bytes 140997120
  1047.3 3.7 collective-permute-start.2
  1051.1 3.5 collective-permute-start.1
  1054.5 2.7 collective-permute-start
  1057.2 4.9 slice.25
  1062.1 3.6 collective-permute-start.3
  1065.7 29.4 %fusion.25 = f32[64,896]{1,0:T(8,128)} fusion(bf16[37984,896]{1,0:T(8,128)(2,1)} %param.7, f32[64,37984]{1,0:T(8,128)} %get-tuple-element.18, bf16[64,37984]{1,0:T(8,128)(2,1)} %param.8, f32[64]{0:T(128)S(1)} %get-tuple-element.12, f32[64]{0:T(128)S(1)} %get-tuple-element.14, f32[64]{0:T(128)S(1)} %get-tuple-element.13, f32[64]{0:T(128)S(1)} %get-tuple-element.15, ...), kind=kOutput, calls=%fused_computation.46 | convolution fusion | flops 4385480704 | bytes 82883840 | tf_op jit(solution)/shard_map/dot_general | solution.py:37
  1095.1 0.0 all-reduce.5.cloned.1.call-update
  1095.2 0.6 dynamic-slice.4
  1096.4 39.6 %all-reduce.5.cloned.1.call-done = f32[64,896]{1,0:T(8,128)} async-done(((f32[64,896]{1,0:T(8,128)}), f32[64,896]{1,0:T(8,128)}) %all-reduce.5.cloned.1.call-update) | async-done | bytes 229392 | tf_op jit(solution)/shard_map/psum | solution.py:37
  1135.9 1.1 fusion.15
  1137.1 330.7 %all-reduce.2 = (f32[]{:T(128)}, f32[896]{0:T(1024)}) all-reduce(f32[]{:T(128)} %get-tuple-element.11, f32[896]{0:T(1024)S(1)} %get-tuple-element.7), channel_id=1, replica_groups=mesh['tp'=4,'dp'=32] {'dp'}, use_global_device_ids=true, to_apply=%region_11.0 | all-reduce | flops 897 | bytes 7176 | tf_op jit(solution)/shard_map/psum | solution.py:34
  1467.8 1.7 fusion.16
  1469.5 0.0 collective-permute-done.3
  1469.5 0.0 collective-permute-done.2
  1469.5 0.0 collective-permute-done.1
  1469.5 101.9 %concatenate = f32[37984,156]{0,1:T(8,128)} concatenate(f32[37984,28]{0,1:T(8,128)} %collective-permute-done.3, f32[37984,32]{0,1:T(8,128)} %collective-permute-done.2, f32[37984,32]{0,1:T(8,128)} %collective-permute-done.1, f32[37984,32]{0,1:T(8,128)} %collective-permute-done, f32[37984,32]{0,1:T(8,128)} %fusion), dimensions={1} | concatenate | bytes 47404032
  1571.4 5.3 constant_dynamic-slice_fusion
  (16 shorter events, 0.1 us)
Async XLA Ops:
  7.2 1128.8 %all-reduce.5.cloned.1.call-start = ((), (), s32[]{:S(2)}) async-start(), calls=%async_computation | async-start | bytes 458752 | tf_op jit(solution)/shard_map/psum | solution.py:37
  8.9 34.3 %copy-start.1 = (f32[64]{0:T(128)}, f32[64]{0:T(128)S(1)}, u32[]{:S(2)}) copy-start(f32[64]{0:T(128)S(1)} %fusion.17) | copy-start | bytes 772
  12.1 40.5 %copy-start.3 = (s32[64]{0:T(128)S(1)}, s32[64]{0:T(128)}, u32[]{:S(2)}) copy-start(s32[64]{0:T(128)} %param.9) | copy-start | bytes 772
  43.3 93.6 %copy-start = (bf16[64,896]{1,0:T(8,128)(2,1)S(1)}, bf16[64,896]{1,0:T(8,128)(2,1)}, u32[]{:S(2)}) copy-start(bf16[64,896]{1,0:T(8,128)(2,1)} %param.5) | copy-start | bytes 344068
  1047.3 422.1 %collective-permute-start.2 = (f32[37984,32]{0,1:T(8,128)}, f32[37984,32]{0,1:T(8,128)}, u32[]{:S(2)}, u32[]{:S(2)}) collective-permute-start(f32[37984,32]{0,1:T(8,128)} %fusion), channel_id=1, source_target_pairs={{0,3},{1,4},{2,5},{3,6},{4,7},{5,8},{6,9},{7,10},{8,11},{9,12},{10... | collective-permute-start | bytes 14585864
  1051.1 418.4 %collective-permute-start.1 = (f32[37984,32]{0,1:T(8,128)}, f32[37984,32]{0,1:T(8,128)}, u32[]{:S(2)}, u32[]{:S(2)}) collective-permute-start(f32[37984,32]{0,1:T(8,128)} %fusion), channel_id=1, source_target_pairs={{0,2},{1,3},{2,4},{3,5},{4,6},{5,7},{6,8},{7,9},{8,10},{9,11},{10,... | collective-permute-start | bytes 14585864
  1054.5 415.0 %collective-permute-start = (f32[37984,32]{0,1:T(8,128)}, f32[37984,32]{0,1:T(8,128)}, u32[]{:S(2)}, u32[]{:S(2)}) collective-permute-start(f32[37984,32]{0,1:T(8,128)} %fusion), channel_id=1, source_target_pairs={{0,1},{1,2},{2,3},{3,4},{4,5},{5,6},{6,7},{7,8},{8,9},{9,10},{10,1... | collective-permute-start | bytes 14585864
  1062.1 33.1 %copy-start.4 = (u32[128]{0:T(128)S(1)}, u32[128]{0:T(128)}, u32[]{:S(2)}) copy-start(u32[128]{0:T(128)} %constant.23) | copy-start | bytes 1540
  1062.1 405.7 %copy-start.2 = (f32[64]{0:T(128)S(1)}, f32[64]{0:T(128)}, u32[]{:S(2)}) copy-start(f32[64]{0:T(128)} %copy-done.1) | copy-start | bytes 772
  1062.1 407.4 %collective-permute-start.3 = (f32[37984,28]{0,1:T(8,128)}, f32[37984,28]{0,1:T(8,128)}, u32[]{:S(2)}, u32[]{:S(2)}) collective-permute-start(f32[37984,28]{0,1:T(8,128)} %slice.25), channel_id=1, source_target_pairs={{0,4},{1,5},{2,6},{3,7},{4,8},{5,9},{6,10},{7,11},{8,12},{9,13},{1... | collective-permute-start | bytes 12762632
Sparse Core Ops, SparseCore 0:
  1095.3 40.6 all-reduce.4
where the time goes:
time: 1590 us; the launch traced here: 1580 us
  blocking collectives  1270 us (80%)
  local copies, waits for them, and re-layouts  113 us (7%)
  matrix products  111 us (7%)
  waiting for transfers between devices  39.6 us (2%)
  other arithmetic  17.4 us (1%)
    unnamed x1, blocking collectives  860 us
    psum x1, blocking collectives, device_fn(): loss_val = lax.psum(jnp.sum(weight * kl_tok), 'dp')  331 us
    unnamed x14, local copies, waits for them, and re-layouts  113 us
    psum x1, blocking collectives, device_fn(): tok_count = lax.psum(jnp.sum(mask_f32), 'dp')  68.6 us
    dot_general x1, matrix products, device_fn(): jnp.einsum('nv,nd->vd', d_raw, normed, preferred_element_type=jnp.float32)  50.7 us
    psum x1, waiting for transfers between devices, device_fn(): lax.psum(jnp.dot(d_raw, emb_loc, preferred_element_type=jnp.float32), 'tp')  39.6 us
  transfers between devices with their start and end apart: 5, of which 1 were waited for; matrix products, arithmetic and copies ran while one was open for 2% of the time, Pallas kernels for 0%

commit v1 on v0

v1 whole, which is shorter than its diff:
```python
import jax
import jax.numpy as jnp
from jax import lax
from jax.sharding import PartitionSpec as P

SOFT_CAP = 30.0
NORM_EPS = 1e-6


def solution(mesh):
    dp_n = mesh.shape['dp']

    def device_fn(hid_loc, norm_w, emb_loc, teach_loc, mask_loc):
        tok, dim = hid_loc.shape
        vloc = emb_loc.shape[0]
        vsub = vloc // dp_n
        dp_i = lax.axis_index('dp')
        x = hid_loc.astype(jnp.float32)
        scale = 1.0 + norm_w.astype(jnp.float32)
        inv = lax.rsqrt(jnp.mean(x * x, axis=-1, keepdims=True) + NORM_EPS)
        xs = x * inv
        xs_all = lax.all_gather(xs, 'dp', axis=0, tiled=True)
        g_all = (xs_all * scale).astype(jnp.bfloat16)

        t32 = teach_loc.astype(jnp.float32)
        t_x = lax.all_to_all(t32, 'dp', split_axis=1, concat_axis=0, tiled=True)
        m_loc = jnp.max(t32, axis=-1)
        t_sh = t32 - m_loc[:, None]
        t_exp = jnp.exp(t_sh)
        tea = lax.all_gather(jnp.stack([m_loc, jnp.sum(t_exp, axis=-1), jnp.sum(t_exp * t_sh, axis=-1)], axis=0), 'tp')
        t_max = jnp.max(tea[:, 0], axis=0)
        shift = tea[:, 0] - t_max
        fac = jnp.exp(shift)
        s_one = jnp.sum(fac * tea[:, 1], axis=0)
        s_two = jnp.sum(fac * (tea[:, 2] + shift * tea[:, 1]), axis=0)
        log_s = jnp.log(s_one)
        neg_ent = s_two / s_one - log_s
        lse_tea = t_max + log_s
        mask_f32 = mask_loc.astype(jnp.float32)
        small = lax.all_gather(jnp.stack([lse_tea, mask_f32], axis=0), 'dp', axis=1, tiled=True)
        weight = small[1] / jnp.sum(small[1])
        lse_all = small[0]

        emb_sub = lax.dynamic_slice_in_dim(emb_loc, dp_i * vsub, vsub, axis=0)
        raw = jnp.einsum('nd,vd->nv', g_all, emb_sub, preferred_element_type=jnp.float32)
        th = jnp.tanh(raw / SOFT_CAP)
        z = SOFT_CAP * th
        e_s = jnp.exp(z)
        sum_s = lax.psum(jnp.sum(e_s, axis=-1), ('tp', 'dp'))
        p_t = jnp.exp(t_x - lse_all[:, None])
        d_raw = ((e_s / sum_s[:, None] - p_t) * weight[:, None] * (1.0 - th * th)).astype(jnp.bfloat16)
        cross = jnp.sum(jnp.sum(p_t * z, axis=-1) * weight)
        demb_t = jnp.einsum('nd,nv->dv', g_all, d_raw, preferred_element_type=jnp.float32)
        grad_emb = lax.all_to_all(demb_t, 'dp', split_axis=0, concat_axis=1, tiled=True).T
        dg_part = jnp.dot(d_raw, emb_sub, preferred_element_type=jnp.float32)
        dg = lax.psum(lax.psum_scatter(dg_part, 'dp', scatter_dimension=0, tiled=True), 'tp')

        w_loc = mask_f32 / jnp.sum(small[1])
        lse_stu = jnp.log(lax.dynamic_slice_in_dim(sum_s, dp_i * tok, tok))
        own = jnp.sum(w_loc * (neg_ent + lse_stu)) / 4.0
        dw_loc = jnp.sum(dg * xs, axis=0)
        dxs = dg * scale
        dx = inv * dxs - x * (inv * inv * inv) * (jnp.sum(dxs * x, axis=-1, keepdims=True) / dim)
        fin = lax.psum(jnp.concatenate([dw_loc / 4.0, (own - cross)[None]]), ('tp', 'dp'))
        return fin[dim], dx.astype(jnp.bfloat16), grad_emb, fin[:dim]

    return jax.shard_map(device_fn, mesh=mesh, in_specs=(P('dp', None), P(None), P('tp', None), P('dp', 'tp'), P('dp')), out_specs=(P(), P('dp', None), P('tp', 'dp'), P(None)), check_vma=False)
```

time: 1590 us -> 555 us (0.35)
  blocking collectives: 1270 us -> 283 us
  waiting for transfers between devices: 39.6 us -> 119 us
  matrix products: 111 us -> 35.6 us
  local copies, waits for them, and re-layouts: 113 us -> 59.5 us
    unnamed x1 -> x0, blocking collectives: 860 us -> none
    psum x3 -> x2, blocking collectives: 405 us -> 131 us  [the longest x1 66.9 us: device_fn(): lax.psum(jnp.concatenate([dw_loc / 4.0, (own - cross)[None]]), ('tp', 'dp'))]
    all_gather x0 -> x2, blocking collectives: none -> 152 us  [the longest x1 141 us: device_fn(): lax.all_gather(jnp.stack([lse_tea, mask_f32], axis=0), 'dp', axis=1, tile...]
    unnamed x14 -> x11, local copies, waits for them, and re-layouts: 113 us -> 2.31 us
    reduce_scatter x0 -> x1, waiting for transfers between devices: none -> 93.4 us  [device_fn(): lax.psum_scatter(dg_part, 'dp', scatter_dimension=0, tiled=True)]
    dot_general x3, matrix products: 111 us -> 35.6 us  [the longest x1 14.4 us: device_fn(): jnp.einsum('nd,vd->nv', g_all, emb_sub, preferred_element_type=jnp.float32)]
    all_to_all x0 -> x6, local copies, waits for them, and re-layouts: none -> 56.7 us  [the longest x3 37.8 us: device_fn(): t_x = lax.all_to_all(t32, 'dp', split_axis=1, concat_axis=0, tiled=True)]
  transfers between devices with their start and end apart: 5 -> 5, of which waited for: 1 -> 2; matrix products, arithmetic and copies ran while one was open for 2% -> 10% of each run, Pallas kernels for 0% -> 0%
where the time goes in v1:
time: 555 us; the launch traced here: 553 us
  blocking collectives  283 us (51%)
  waiting for transfers between devices  119 us (21%)
  local copies, waits for them, and re-layouts  59.5 us (11%)
  matrix products  35.6 us (6%)
  other arithmetic  25.3 us (5%)
  starting transfers between devices  15.5 us (3%)
  between operations  15.2 us (3%)
    all_gather x1, blocking collectives, device_fn(): lax.all_gather(jnp.stack([lse_tea, mask_f32], axis=0), 'dp', axis=1, tile...  141 us
    reduce_scatter x1, waiting for transfers between devices, device_fn(): lax.psum_scatter(dg_part, 'dp', scatter_dimension=0, tiled=True)  93.4 us
    psum x1, blocking collectives, device_fn(): lax.psum(jnp.concatenate([dw_loc / 4.0, (own - cross)[None]]), ('tp', 'dp'))  66.9 us
    psum x1, blocking collectives, device_fn(): sum_s = lax.psum(jnp.sum(e_s, axis=-1), ('tp', 'dp'))  64.2 us
    all_to_all x3, local copies, waits for them, and re-layouts, device_fn(): t_x = lax.all_to_all(t32, 'dp', split_axis=1, concat_axis=0, tiled=True)  37.8 us
    psum x1, waiting for transfers between devices, device_fn(): lax.psum(lax.psum_scatter(dg_part, 'dp', scatter_dimension=0, tiled=True)...  25.9 us
    all_to_all x3, local copies, waits for them, and re-layouts, device_fn(): lax.all_to_all(demb_t, 'dp', split_axis=0, concat_axis=1, tiled=True)  18.9 us
    dot_general x1, matrix products, device_fn(): jnp.einsum('nd,vd->nv', g_all, emb_sub, preferred_element_type=jnp.float32)  14.4 us
  transfers between devices with their start and end apart: 5, of which 2 were waited for; matrix products, arithmetic and copies ran while one was open for 10% of the time, Pallas kernels for 0%

profile of v1, /device:TPU:1, one launch (start us, length us, event | category | flops | bytes accessed | tf_op | source)
XLA Modules:
  0.0 553.2 jit_solution(1808824601778598815)
XLA Ops:
  7.2 1.0 fusion.5
  8.2 1.7 convert_multiply_fusion.2
  10.0 12.9 %all_to_all.28 = f32[64,32,1187]{2,1,0:T(8,128)} reshape(bf16[64,37984]{1,0:T(8,128)(2,1)} %param.8) | data formatting | bytes 14585856 | tf_op jit(solution)/shard_map/all_to_all | solution.py:26
  22.9 13.9 %copy.26 = f32[64,32,1187]{2,0,1:T(8,128)} copy(f32[64,32,1187]{2,1,0:T(8,128)} %all_to_all.28) | data formatting | bytes 19447808 | tf_op jit(solution)/shard_map/all_to_all | solution.py:26
  36.8 9.7 %all-to-all-start = ((f32[64,32,1187]{2,0,1:T(8,128)}), f32[64,32,1187]{2,0,1:T(8,128)}, u32[]{:S(2)}, u32[]{:S(2)}) async-start(f32[64,32,1187]{2,0,1:T(8,128)} %copy.26), calls=%async_computation | async-start | bytes 20971520 | tf_op jit(solution)/shard_map/all_to_all | solution.py:26
  46.5 3.1 reduce_max.27
  49.6 4.7 exponential_reduce_fusion
  54.4 10.5 %all-gather.1 = f32[4,3,64]{2,1,0:T(4,128)S(1)} all-gather(f32[1,3,64]{2,1,0:T(4,128)S(1)} %maximum_bitcast_fusion), channel_id=2, replica_groups=mesh['tp'=4,'dp'=32] {'tp'}, dimensions={0}, use_global_device_ids=true | all-gather | bytes 3840 | tf_op jit(solution)/shard_map/all_gather | solution.py:30
  65.0 141.1 %all-gather.2 = f32[32,64,2]{1,2,0:T(2,128)S(1)} all-gather(f32[1,64,2]{1,2,0:T(2,128)S(1)} %maximum_bitcast_fusion.1), channel_id=1, replica_groups=mesh['tp'=4,'dp'=32] {'dp'}, dimensions={0}, use_global_device_ids=true | all-gather | bytes 16896 | tf_op jit(solution)/shard_map/all_gather | solution.py:40
  206.1 0.1 reshape.76
  206.2 0.6 slice_reduce_fusion
  206.8 0.7 slice_divide_fusion
  207.5 11.0 %copy.29 = f32[2048,1187]{0,1:T(8,128)} copy(f32[2048,1187]{1,0:T(8,128)} %bitcast.1) | data formatting | bytes 19447808 | tf_op jit(solution)/shard_map/all_to_all | solution.py:26
  218.4 14.4 %multiply_reduce_fusion = (f32[2048]{0:T(1024)S(1)}, f32[2048]{0:T(1024)S(1)}, f32[2048,1187]{0,1:T(8,128)}) fusion(f32[2048,1187]{0,1:T(8,128)} %copy.29, f32[2048]{0:T(1024)S(1)} %bitcast.41, bf16[37984,896]{1,0:T(8,128)(2,1)} %param.7, s32[]{:T(128)S(6)} %select_n.6, f32[2048,896]{1,0:T(8,128)} %all-gather.5.cloned.1.call-done, f32[896]{0:T(1024)S(1)} %convert_add_fusion), kind=kOutput, calls=%fused_computation.2 | convolution fusion | flops 4374560768 | bytes 28993028 | tf_op jit(solution)/shard_map/nd,vd->nv/dot_general | solution.py:45
  232.9 64.2 %psum.21 = f32[2048]{0:T(1024)S(1)} all-reduce(f32[2048]{0:T(1024)S(1)} %get-tuple-element.5), channel_id=1, replica_groups=mesh['tp'=4,'dp'=32] {'tp','dp'}, use_global_device_ids=true, to_apply=%region_2.0 | all-reduce | flops 2048 | bytes 16384 | tf_op jit(solution)/shard_map/psum | solution.py:49
  297.1 8.6 %multiply_convert_fusion = bf16[2048,1187]{0,1:T(8,128)(2,1)S(1)} fusion(f32[2048,1187]{0,1:T(8,128)} %get-tuple-element.21, f32[2048,1187]{0,1:T(8,128)} %copy.29, f32[2048]{0:T(1024)S(1)} %bitcast.39, f32[2048]{0:T(1024)S(1)} %bitcast.42, f32[2048]{0:T(1024)S(1)} %psum.21), kind=kLoop, calls=%fused_computation.3 | loop fusion | flops 21878784 | bytes 24334336 | tf_op jit(solution)/shard_map/convert_element_type | solution.py:51
  305.7 2.2 copy-done
  307.9 9.5 %fusion.1 = f32[2048,896]{1,0:T(8,128)} fusion(bf16[2048,1187]{0,1:T(8,128)(2,1)S(1)} %multiply_convert_fusion, bf16[37984,896]{1,0:T(8,128)(2,1)} %param.7, s32[]{:T(128)S(6)} %select_n.6), kind=kOutput, calls=%fused_computation.9 | convolution fusion | flops 4356308992 | bytes 14338052 | tf_op jit(solution)/shard_map/dot_general | solution.py:55
  317.4 11.7 %fusion.4 = f32[896,1187]{1,0:T(8,128)} fusion(bf16[2048,1187]{0,1:T(8,128)(2,1)} %copy-done, f32[2048,896]{1,0:T(8,128)} %all-gather.5.cloned.1.call-done, f32[896]{0:T(1024)S(1)} %convert_add_fusion), kind=kOutput, calls=%fused_computation.12 | convolution fusion | flops 4359979008 | bytes 16459776 | tf_op jit(solution)/shard_map/nd,nv->dv/dot_general | solution.py:53
  329.1 5.2 all_to_all.32
  334.3 5.5 %all-to-all-start.1 = ((f32[32,28,1187]{2,1,0:T(8,128)}), f32[32,28,1187]{2,1,0:T(8,128)}, u32[]{:S(2)}, u32[]{:S(2)}) async-start(f32[32,28,1187]{2,1,0:T(8,128)} %all_to_all.32), calls=%async_computation.2 | async-start | bytes 10485760 | tf_op jit(solution)/shard_map/all_to_all | solution.py:54
  339.8 0.3 all-reduce.2.cloned.1.call-start
  340.1 93.4 %reduce-scatter.2.cloned.1.call-done = f32[64,896]{1,0:T(8,128)} async-done(((f32[2048,896]{1,0:T(8,128)}), f32[64,896]{1,0:T(8,128)}) %reduce-scatter.2.cloned.1.call-update) | async-done | bytes 229392 | tf_op jit(solution)/shard_map/reduce_scatter | solution.py:56
  433.5 1.4 fusion.10
  435.5 0.6 multiply_reduce_fusion.2
  436.8 7.2 %copy.32 = f32[28,32,1187]{2,1,0:T(8,128)} copy(f32[28,32,1187]{2,0,1:T(8,128)} %bitcast.18) | data formatting | bytes 8508416 | tf_op jit(solution)/shard_map/all_to_all | solution.py:54
  444.0 6.5 %all_to_all.35 = f32[28,37984]{1,0:T(8,128)} reshape(f32[28,32,1187]{2,1,0:T(8,128)} %copy.32) | data formatting | bytes 8508416 | tf_op jit(solution)/shard_map/all_to_all | solution.py:54
  450.5 25.9 %all-reduce.2.cloned.1.call-done = f32[64,896]{1,0:T(8,128)} async-done(((f32[64,896]{1,0:T(8,128)}), f32[64,896]{1,0:T(8,128)}) %all-reduce.2.cloned.1.call-update) | async-done | bytes 229392 | tf_op jit(solution)/shard_map/psum | solution.py:56
  476.4 1.1 fusion.9
  477.6 66.9 %psum.23 = f32[897]{0:T(1024)S(1)} all-reduce(f32[897]{0:T(1024)S(1)} %pad_maximum_fusion), channel_id=1, replica_groups=mesh['tp'=4,'dp'=32] {'tp','dp'}, use_global_device_ids=true, to_apply=%region_16.0 | all-reduce | flops 897 | bytes 7176 | tf_op jit(solution)/shard_map/psum | solution.py:64
  544.5 0.5 slice.30
  545.0 1.7 fusion.8
  (31 shorter events, 0.3 us)
Async XLA Ops:
  7.2 211.3 %all-gather.5.cloned.1.call-start = ((), (), s32[]{:S(2)}) async-start(), calls=%async_computation.3 | async-start | bytes 7569408 | tf_op jit(solution)/shard_map/all_gather | solution.py:22
  36.8 170.7 %all-to-all-start = ((f32[64,32,1187]{2,0,1:T(8,128)}), f32[64,32,1187]{2,0,1:T(8,128)}, u32[]{:S(2)}, u32[]{:S(2)}) async-start(f32[64,32,1187]{2,0,1:T(8,128)} %copy.26), calls=%async_computation | async-start | bytes 20971520 | tf_op jit(solution)/shard_map/all_to_all | solution.py:26
  46.4 18.5 %copy-start.4 = (s32[64]{0:T(128)S(1)}, s32[64]{0:T(128)}, u32[]{:S(2)}) copy-start(s32[64]{0:T(128)} %param.9) | copy-start | bytes 772
  46.5 160.3 %copy-start.3 = (bf16[896]{0:T(1024)(128)(2,1)S(1)}, bf16[896]{0:T(1024)(128)(2,1)}, u32[]{:S(2)}) copy-start(bf16[896]{0:T(1024)(128)(2,1)} %param.6) | copy-start | bytes 5380
  46.5 387.0 %reduce-scatter.2.cloned.1.call-start = ((), (), s32[]{:S(2)}) async-start(), calls=%async_computation.4 | async-start | bytes 7569408 | tf_op jit(solution)/shard_map/reduce_scatter | solution.py:56
  305.7 2.2 copy-start
  334.3 102.5 %all-to-all-start.1 = ((f32[32,28,1187]{2,1,0:T(8,128)}), f32[32,28,1187]{2,1,0:T(8,128)}, u32[]{:S(2)}, u32[]{:S(2)}) async-start(f32[32,28,1187]{2,1,0:T(8,128)} %all_to_all.32), calls=%async_computation.2 | async-start | bytes 10485760 | tf_op jit(solution)/shard_map/all_to_all | solution.py:54
  339.8 136.6 %all-reduce.2.cloned.1.call-start = ((), (), s32[]{:S(2)}) async-start(), calls=%async_computation.5 | async-start | bytes 458752 | tf_op jit(solution)/shard_map/psum | solution.py:56
  433.5 42.9 %copy-start.1 = (bf16[64,896]{1,0:T(8,128)(2,1)S(1)}, bf16[64,896]{1,0:T(8,128)(2,1)}, u32[]{:S(2)}) copy-start(bf16[64,896]{1,0:T(8,128)(2,1)} %param.5) | copy-start | bytes 344068
  544.5 2.2 copy-start.2
Sparse Core Ops, SparseCore 0:
  10.8 137.3 all-gather.4
  317.5 115.9 reduce-scatter.1
  435.8 40.5 all-reduce.1

commit v2 on v0

v2 whole, which is shorter than its diff:
```python
import functools

import jax
import jax.numpy as jnp
from jax import lax
from jax.experimental import pallas as pl
from jax.experimental.pallas import tpu as pltpu
from jax.sharding import PartitionSpec as P

SOFT_CAP = 30.0
NORM_EPS = 1e-6
SUB = 256
SLOTS = 3
MESH = pl.DeviceIdType.MESH
NT = (((1,), (1,)), ((), ()))
NN = (((1,), (0,)), ((), ()))


def body(cfg, hid, nw, mask, emb, teach, o_emb, o_dh, o_dw, gbuf,
         t_stage, th_buf, t_recv, tb, e_slot, e_sub, g_all, g_t, gin, dr_loc, r_blk, dr_blk, de_st,
         m_buf, acc, st_tp, st_t, st_dp, st_all, dg_tp, dw_dp, xs_buf, gl_buf,
         tb_sem, es_sem, sub_sem, gl_sem, gin_sem, loc_sem, snd_s, rcv_s, t_snd, t_rcv, de_snd, de_rcv):
    tp_n, dp_n, ny = cfg
    tok, dim = hid.shape
    vloc = emb.shape[0]
    win = t_recv.shape[2]
    n_sub = win // SUB
    n_ch = t_stage.shape[1] // win
    tail = vloc - (n_ch - 1) * win
    chips = dp_n // 2
    nz = chips // ny
    rq = tok // tp_n
    cpad = de_st.shape[1] // dp_n
    cols = dim // dp_n
    last = n_ch - 1
    tp_i = lax.axis_index('tp')
    dp_i = lax.axis_index('dp')
    chip = dp_i // 2
    core = dp_i % 2

    def peer_chip(k):
        j = (k * 5) % chips
        return ((chip // ny + j // ny) % nz) * ny + (chip % ny + j % ny) % ny

    def peer(k):
        return peer_chip(k // 2) * 2 + (core + k % 2) % 2

    def active(dev, s):
        return dev * win + s * SUB < vloc

    def n_act(s):
        return sum(1 for d in range(dp_n) if d * win + s * SUB < vloc)

    barrier = pltpu.get_barrier_semaphore()

    @pl.loop(1, dp_n)
    def _(k):
        pl.semaphore_signal(barrier, inc=1, device_id={'dp': peer(k)}, device_id_type=MESH)

    @pl.loop(1, tp_n)
    def _(k):
        pl.semaphore_signal(barrier, inc=1, device_id={'tp': (tp_i + k) % tp_n}, device_id_type=MESH)

    def tb_copy(r):
        return pltpu.make_async_copy(teach.at[pl.ds(r * 16, 16)], tb.at[r % 2], tb_sem.at[r % 2])

    tb_copy(0).start()
    tb_copy(1).start()

    def e_copy(i, slot, rows):
        return pltpu.make_async_copy(emb.at[pl.ds(pl.multiple_of(i * win, 16), rows)],
                                     e_slot.at[slot, pl.ds(0, rows)], es_sem.at[slot])

    def e_start(i):
        @pl.when(i < last)
        def _():
            e_copy(i, i % SLOTS, win).start()

        @pl.when(i == last)
        def _():
            e_copy(i, i % SLOTS, tail).start()

    def e_wait(i):
        @pl.when(i < last)
        def _():
            e_copy(i, i % SLOTS, win).wait()

        @pl.when(i == last)
        def _():
            e_copy(i, i % SLOTS, tail).wait()

    def sub_copy(rows):
        return pltpu.make_async_copy(emb.at[pl.ds(pl.multiple_of(dp_i * win, 16), rows)],
                                     e_sub.at[pl.ds(0, rows)], sub_sem)

    @pl.when(dp_i < last)
    def _():
        sub_copy(win).start()

    @pl.when(dp_i == last)
    def _():
        sub_copy(tail).start()

    x = hid[...].astype(jnp.float32)
    scale = 1.0 + nw[...].astype(jnp.float32)
    inv = lax.rsqrt(jnp.mean(x * x, axis=-1, keepdims=True) + NORM_EPS)
    xs = x * inv
    xs_buf[...] = xs.reshape(tp_n, rq, dim)
    gl_buf[...] = (xs * scale).astype(jnp.bfloat16)

    own_g = pltpu.make_async_copy(xs_buf.at[tp_i], gbuf.at[chip, core, tp_i], gl_sem)
    own_g.start()

    pl.semaphore_wait(barrier, dp_n - 1 + tp_n - 1)

    pieces = [(c0, min(1024, vloc - c0)) for c0 in range(0, vloc, 1024)]
    full_p = vloc // 1024

    t_stage[:, pl.ds(vloc // 128 * 128, n_ch * win - vloc // 128 * 128)] = jnp.zeros(
        (tok, n_ch * win - vloc // 128 * 128), jnp.float32)
    for r in range(tok // 16):
        tb_copy(r).wait()
        rows = pl.ds(r * 16, 16)

        def conv(c0, width, mx):
            v = tb[r % 2, :, pl.ds(c0, width)].astype(jnp.float32)
            t_stage[rows, pl.ds(c0, width)] = v
            return v

        def step(i, mx):
            v = conv(pl.multiple_of(i * 1024, 128), 1024, mx)
            for q in range(8):
                mx = jnp.maximum(mx, v[:, q * 128:(q + 1) * 128])
            return mx

        mx = lax.fori_loop(0, full_p, step, jnp.full((16, 128), -jnp.inf, jnp.float32))
        m1 = jnp.max(mx, axis=-1, keepdims=True)
        if full_p * 1024 < vloc:
            v = conv(full_p * 1024, vloc - full_p * 1024, None)
            m1 = jnp.maximum(m1, jnp.max(v, axis=-1, keepdims=True))
        m_buf[rows, :] = jnp.broadcast_to(m1, (16, 128))
        if r + 2 < tok // 16:
            tb_copy(r + 2).start()

    for i in range(SLOTS):
        e_start(i)

    def ga_copy(pc):
        return pltpu.make_async_remote_copy(xs_buf.at[tp_i], gbuf.at[chip, core, tp_i], snd_s.at[0], rcv_s.at[0],
                                            device_id={'dp': pc * 2 + core}, device_id_type=MESH)

    @pl.loop(1, chips)
    def _(k):
        ga_copy(peer_chip(k)).start()

    def t_copy(dev, s):
        lane = pl.multiple_of(dev * win + s * SUB, SUB)
        return pltpu.make_async_remote_copy(t_stage.at[:, pl.ds(lane, SUB)], t_recv.at[dp_i, :, pl.ds(s * SUB, SUB)],
                                            t_snd.at[s], t_rcv.at[s], device_id={'dp': dev}, device_id_type=MESH)

    for s in range(n_sub):
        @pl.loop(1, dp_n)
        def _(k, s=s):
            dev = peer(k)

            @pl.when(active(dev, s))
            def _():
                t_copy(dev, s).start()

        @pl.when(active(dp_i, s))
        def _(s=s):
            lane = pl.multiple_of(dp_i * win + s * SUB, SUB)
            t_recv[dp_i, :, pl.ds(s * SUB, SUB)] = t_stage[:, pl.ds(lane, SUB)]

    own_g.wait()
    pltpu.make_async_remote_copy(gbuf.at[pl.ds(0, chips - 1), 0, 0], gbuf.at[pl.ds(0, chips - 1), 0, 0], snd_s.at[0],
                                 rcv_s.at[0], device_id={'dp': dp_i}, device_id_type=MESH).wait_recv()

    def gb_copy(q):
        return pltpu.make_async_remote_copy(gbuf.at[:, core, tp_i], gbuf.at[:, core, tp_i], snd_s.at[1],
                                            rcv_s.at[1], device_id={'tp': q}, device_id_type=MESH)

    @pl.loop(1, tp_n)
    def _(k):
        gb_copy((tp_i + k) % tp_n).start()

    acc[...] = jnp.zeros_like(acc)
    lanes = lax.broadcasted_iota(jnp.int32, (tok, 128), 1)

    @pl.loop(0, n_ch)
    def _(i):
        e_wait(i)
        base = pl.multiple_of(i * win, SUB)
        th_buf[:, pl.ds(base, win)] = lax.dot_general(gl_buf[...], e_slot[i % SLOTS], NT,
                                                      preferred_element_type=jnp.float32)

        @pl.when(i + SLOTS < n_ch)
        def _():
            e_start(i + SLOTS)

        m_l = m_buf[...]
        a_s, a_1, a_2, a_x = acc[0], acc[1], acc[2], acc[3]
        for q in range(win // 128):
            at = pl.ds(pl.multiple_of(base + q * 128, 128), 128)
            th = jnp.tanh(th_buf[:, at] * (1.0 / SOFT_CAP))
            th_buf[:, at] = th
            z = SOFT_CAP * th
            ok = base + q * 128 + lanes < vloc
            e_s = jnp.where(ok, jnp.exp(z), 0.0)
            sh = t_stage[:, at] - m_l
            e_t = jnp.where(ok, jnp.exp(sh), 0.0)
            sh = jnp.where(ok, sh, 0.0)
            a_s = a_s + e_s
            a_1 = a_1 + e_t
            a_2 = a_2 + e_t * sh
            a_x = a_x + e_t * jnp.where(ok, z, 0.0)
        acc[0] = a_s
        acc[1] = a_1
        acc[2] = a_2
        acc[3] = a_x

    for i in range(SLOTS):
        e_start(i)

    parts = [m_buf[:, 0:1]] + [jnp.sum(acc[j], axis=-1, keepdims=True) for j in (1, 2, 3, 0)]
    tile = jnp.zeros((tok, 128), jnp.float32)
    for j, v in enumerate(parts):
        tile = jnp.where(lanes == j, v, tile)
    st_tp[tp_i] = tile

    def st_copy(q):
        return pltpu.make_async_remote_copy(st_tp.at[tp_i], st_tp.at[tp_i], snd_s.at[2], rcv_s.at[2],
                                            device_id={'tp': q}, device_id_type=MESH)

    @pl.loop(1, tp_n)
    def _(k):
        st_copy((tp_i + k) % tp_n).start()

    sib = chip * 2 + (core + 1) % 2
    gb_wait = pltpu.make_async_remote_copy(gbuf.at[:, 0, pl.ds(0, tp_n - 1)], gbuf.at[:, 0, pl.ds(0, tp_n - 1)],
                                           snd_s.at[1], rcv_s.at[1], device_id={'dp': dp_i}, device_id_type=MESH)
    gb_wait.wait_recv()
    gc_copy = pltpu.make_async_remote_copy(gbuf.at[:, core], gbuf.at[:, core], snd_s.at[3], rcv_s.at[3],
                                           device_id={'dp': sib}, device_id_type=MESH)
    gc_copy.start()

    st_wait = pltpu.make_async_remote_copy(st_tp.at[pl.ds(0, tp_n - 1)], st_tp.at[pl.ds(0, tp_n - 1)], snd_s.at[2],
                                           rcv_s.at[2], device_id={'dp': dp_i}, device_id_type=MESH)
    st_wait.wait_recv()
    t_max = st_tp[0][:, 0:1]
    for q in range(1, tp_n):
        t_max = jnp.maximum(t_max, st_tp[q][:, 0:1])
    s_1 = s_2 = s_x = s_s = jnp.zeros((tok, 1), jnp.float32)
    for q in range(tp_n):
        v = st_tp[q]
        shift = v[:, 0:1] - t_max
        fac = jnp.exp(shift)
        s_1 = s_1 + fac * v[:, 1:2]
        s_2 = s_2 + fac * (v[:, 2:3] + shift * v[:, 1:2])
        s_x = s_x + fac * v[:, 3:4]
        s_s = s_s + v[:, 4:5]
    log_1 = jnp.log(s_1)
    kl = (s_2 - s_x) / s_1 - log_1 + jnp.log(s_s)
    lse_t = t_max + log_1
    inv_s = 1.0 / s_s
    m_loc = mask[...]
    tile = jnp.where(lanes == 0, lse_t, jnp.where(lanes == 1, inv_s, jnp.where(lanes == 2, m_loc, 0.0)))
    tile = jnp.concatenate([tile, jnp.zeros((128 - tok, 128), jnp.float32)], axis=0).T
    st_dp[dp_i] = tile[0:8]

    def sd_copy(dev):
        return pltpu.make_async_remote_copy(st_dp.at[dp_i], st_dp.at[dp_i], snd_s.at[4], rcv_s.at[4],
                                            device_id={'dp': dev}, device_id_type=MESH)

    @pl.loop(1, dp_n)
    def _(k):
        sd_copy(peer(k)).start()

    sd_wait = pltpu.make_async_remote_copy(st_dp.at[pl.ds(0, dp_n - 1)], st_dp.at[pl.ds(0, dp_n - 1)], snd_s.at[4],
                                           rcv_s.at[4], device_id={'dp': dp_i}, device_id_type=MESH)
    sd_wait.wait_recv()
    m_cnt = jnp.sum(jnp.sum(st_dp[...], axis=0)[2:3, :], axis=-1, keepdims=True)
    w_loc = m_loc / m_cnt

    @pl.loop(0, dp_n)
    def _(d):
        v = jnp.concatenate([st_dp[d], jnp.zeros((120, 128), jnp.float32)], axis=0).T
        st_all[d] = v[0:tok]

    dg_tp[tp_i] = jnp.zeros((tok, dim), jnp.float32)

    @pl.loop(0, n_ch)
    def _(i):
        e_wait(i)
        base = pl.multiple_of(i * win, SUB)
        for q in range(win // 128):
            at = pl.ds(pl.multiple_of(base + q * 128, 128), 128)
            th = th_buf[:, at]
            p_s = jnp.exp(SOFT_CAP * th) * inv_s
            p_t = jnp.exp(t_stage[:, at] - lse_t)
            d = (p_s - p_t) * w_loc * (1.0 - th * th)
            ok = base + q * 128 + lanes < vloc
            dr_loc[:, pl.ds(q * 128, 128)] = jnp.where(ok, d, 0.0).astype(jnp.bfloat16)
        dg_tp[tp_i] += lax.dot_general(dr_loc[...], e_slot[i % SLOTS], NN, preferred_element_type=jnp.float32)

        @pl.when(i + SLOTS < n_ch)
        def _():
            e_start(i + SLOTS)

    def dg_copy(q):
        return pltpu.make_async_remote_copy(dg_tp.at[tp_i], dg_tp.at[tp_i], snd_s.at[5], rcv_s.at[5],
                                            device_id={'tp': q}, device_id_type=MESH)

    @pl.loop(1, tp_n)
    def _(k):
        dg_copy((tp_i + k) % tp_n).start()

    gc_copy.wait()

    def gin_copy(d):
        return pltpu.make_async_copy(gbuf.at[d // 2, d % 2], gin.at[d % 2], gin_sem.at[d % 2])

    gin_copy(0).start()
    gin_copy(1).start()

    for d in range(dp_n):
        gin_copy(d).wait()
        gv = (gin[d % 2].reshape(tok, dim) * scale)
        g_all[pl.ds(d * tok, tok), :] = gv.astype(jnp.bfloat16)
        if d + 2 < dp_n:
            gin_copy(d + 2).start()

    for d in range(0, dp_n, 2):
        gv = g_all[pl.ds(d * tok, 2 * tok), :].astype(jnp.float32).T
        for c in range(dp_n):
            gc = gv[c * cols:(c + 1) * cols]
            if cpad != cols:
                gc = jnp.concatenate([gc, jnp.zeros((cpad - cols, 2 * tok), jnp.float32)], axis=0)
            g_t[pl.ds(c * cpad, cpad), pl.ds(d * tok, 2 * tok)] = gc.astype(jnp.bfloat16)

    dg_wait = pltpu.make_async_remote_copy(dg_tp.at[pl.ds(0, tp_n - 1)], dg_tp.at[pl.ds(0, tp_n - 1)], snd_s.at[5],
                                           rcv_s.at[5], device_id={'dp': dp_i}, device_id_type=MESH)
    dg_wait.wait_recv()
    dg = dg_tp[0]
    for q in range(1, tp_n):
        dg = dg + dg_tp[q]
    x = hid[...].astype(jnp.float32)
    inv = lax.rsqrt(jnp.mean(x * x, axis=-1, keepdims=True) + NORM_EPS)
    dxs = dg * scale
    o_dh[...] = (inv * dxs - x * (inv * inv * inv * (jnp.sum(dxs * x, axis=-1, keepdims=True) / dim))).astype(jnp.bfloat16)
    dw = jnp.sum(dg * (x * inv), axis=0, keepdims=True)
    dw_dp[dp_i] = jnp.broadcast_to(jnp.sum(w_loc * kl, axis=0, keepdims=True), (8, 128))
    for j in range(dim // 128):
        dw_dp[dp_i, pl.ds(j, 1), :] = dw[:, j * 128:(j + 1) * 128]

    def dw_copy(dev):
        return pltpu.make_async_remote_copy(dw_dp.at[dp_i], dw_dp.at[dp_i], snd_s.at[6], rcv_s.at[6],
                                            device_id={'dp': dev}, device_id_type=MESH)

    @pl.loop(1, dp_n)
    def _(k):
        dw_copy(peer(k)).start()

    @pl.when(dp_i < last)
    def _():
        sub_copy(win).wait()

    @pl.when(dp_i == last)
    def _():
        sub_copy(tail).wait()

    row_n = 4 * tok

    def de_copy(dev, s):
        lane = pl.multiple_of(dp_i * win + s * SUB, SUB)
        return pltpu.make_async_remote_copy(de_st.at[s % 2, pl.ds(pl.multiple_of(dev * cpad, 8), cpad)],
                                            o_emb.at[:, pl.ds(lane, SUB)], de_snd.at[s % 2], de_rcv,
                                            device_id={'dp': dev}, device_id_type=MESH)

    def de_local(s):
        lane = pl.multiple_of(dp_i * win + s * SUB, SUB)
        return pltpu.make_async_copy(de_st.at[s % 2, pl.ds(pl.multiple_of(dp_i * cpad, 8), cpad)],
                                     o_emb.at[:, pl.ds(lane, SUB)], loc_sem.at[s % 2])

    def de_wait(s):
        @pl.when(active(dp_i, s))
        def _():
            pltpu.make_async_remote_copy(de_st.at[s % 2, pl.ds(0, (dp_n - 1) * cpad)],
                                         de_st.at[s % 2, pl.ds(0, (dp_n - 1) * cpad)], de_snd.at[s % 2], de_rcv,
                                         device_id={'dp': dp_i}, device_id_type=MESH).wait_send()
            de_local(s).wait()

    for s in range(n_sub):
        if s >= 2:
            de_wait(s - 2)

        @pl.when(active(dp_i, s))
        def _(s=s):
            part = t_recv.at[pl.ds(0, dp_n - 1), :, pl.ds(s * SUB, SUB)]
            pltpu.make_async_remote_copy(part, part, t_snd.at[s], t_rcv.at[s], device_id={'dp': dp_i},
                                         device_id_type=MESH).wait_recv()

            @pl.loop(0, dp_n // 4)
            def _(b):
                rows = pl.ds(pl.multiple_of(b * row_n, row_n), row_n)
                r_blk[...] = lax.dot_general(g_all[rows, :], e_sub[pl.ds(s * SUB, SUB), :], NT,
                                             preferred_element_type=jnp.float32)
                for q in range(row_n // 32):
                    d = b * 4 + q * 32 // tok
                    off = q * 32 % tok
                    th = jnp.tanh(r_blk[pl.ds(q * 32, 32), :] * (1.0 / SOFT_CAP))
                    sv = st_all[d, pl.ds(off, 32), :]
                    p_s = jnp.exp(SOFT_CAP * th) * sv[:, 1:2]
                    p_t = jnp.exp(t_recv[d, pl.ds(off, 32), pl.ds(s * SUB, SUB)] - sv[:, 0:1])
                    dv = (p_s - p_t) * (sv[:, 2:3] / m_cnt) * (1.0 - th * th)
                    dr_blk[pl.ds(pl.multiple_of(b * row_n + q * 32, 32), 32), :] = dv.astype(jnp.bfloat16)

            @pl.loop(0, de_st.shape[1] // 256)
            def _(b):
                rows = pl.ds(pl.multiple_of(b * 256, 256), 256)
                de_st[s % 2, rows, :] = lax.dot_general(g_t[rows, :], dr_blk[...], NN,
                                                        preferred_element_type=jnp.float32)

            @pl.loop(1, dp_n)
            def _(k):
                de_copy(peer(k), s).start()

            de_local(s).start()

    dw_wait = pltpu.make_async_remote_copy(dw_dp.at[pl.ds(0, dp_n - 1)], dw_dp.at[pl.ds(0, dp_n - 1)], snd_s.at[6],
                                           rcv_s.at[6], device_id={'dp': dp_i}, device_id_type=MESH)
    dw_wait.wait_recv()
    tot = dw_dp[0]
    for d in range(1, dp_n):
        tot = tot + dw_dp[d]
    o_dw[...] = tot

    ga_wait = pltpu.make_async_remote_copy(gbuf.at[pl.ds(0, chips - 1), 0, 0], gbuf.at[pl.ds(0, chips - 1), 0, 0],
                                           snd_s.at[0], rcv_s.at[0], device_id={'dp': dp_i}, device_id_type=MESH)
    for w in (ga_wait, gb_wait, st_wait, sd_wait, dg_wait, dw_wait):
        w.wait_send()

    def t_drain(s, n):
        pltpu.make_async_remote_copy(t_stage.at[:, pl.ds(0, n * SUB)], t_stage.at[:, pl.ds(0, n * SUB)], t_snd.at[s],
                                     t_rcv.at[s], device_id={'dp': dp_i}, device_id_type=MESH).wait_send()

    for s in range(n_sub):
        @pl.when(active(dp_i, s))
        def _(s=s):
            t_drain(s, n_act(s) - 1)

        @pl.when(jnp.logical_not(active(dp_i, s)))
        def _(s=s):
            t_drain(s, n_act(s))

    for s in range(max(0, n_sub - 2), n_sub):
        de_wait(s)

    total = sum(n_act(s) for s in range(n_sub))
    tail_n = -(-tail // SUB)

    def de_drain(n):
        part = o_emb.at[:, pl.ds(0, n * SUB)]
        pltpu.make_async_remote_copy(part, part, de_snd.at[0], de_rcv, device_id={'dp': dp_i},
                                     device_id_type=MESH).wait_recv()

    @pl.when(dp_i < last)
    def _():
        de_drain(total - n_sub)

    @pl.when(dp_i == last)
    def _():
        de_drain(total - tail_n)

    @pl.when(dp_i > last)
    def _():
        de_drain(total)


def solution(mesh):
    tp_n, dp_n = mesh.shape['tp'], mesh.shape['dp']
    ny = 4 if dp_n >= 32 else 1

    def device_fn(hid_loc, norm_w, emb_loc, teach_loc, mask_loc):
        tok, dim = hid_loc.shape
        vloc = emb_loc.shape[0]
        win = -(-vloc // (dp_n * SUB)) * SUB
        n_ch = -(-vloc // win)
        cols = dim // dp_n
        cpad = -(-cols // 8) * 8
        rq = tok // tp_n
        f32, bf16 = jnp.float32, jnp.bfloat16
        vm, dma = pltpu.VMEM, pltpu.SemaphoreType.DMA
        any_s, vm_s = pl.BlockSpec(memory_space=pl.ANY), pl.BlockSpec(memory_space=pltpu.VMEM)
        wide = n_ch * win
        o_emb, o_dh, o_dw, _ = pl.pallas_call(
            functools.partial(body, (tp_n, dp_n, ny)),
            out_shape=(jax.ShapeDtypeStruct((cpad, wide), f32), jax.ShapeDtypeStruct((tok, dim), bf16),
                       jax.ShapeDtypeStruct((8, 128), f32),
                       jax.ShapeDtypeStruct((dp_n // 2, 2, tp_n, rq, dim), f32)),
            in_specs=[vm_s, vm_s, vm_s, any_s, any_s],
            out_specs=(any_s, vm_s, vm_s, any_s),
            scratch_shapes=[
                vm((tok, wide), f32), vm((tok, wide), f32), vm((dp_n, tok, win), f32), vm((2, 16, vloc), bf16),
                vm((SLOTS, win, dim), bf16), vm((win, dim), bf16), vm((dp_n * tok, dim), bf16),
                vm((dp_n * cpad, dp_n * tok), bf16), vm((2, tp_n, rq, dim), f32), vm((tok, win), bf16),
                vm((4 * tok, SUB), f32), vm((dp_n * tok, SUB), bf16), vm((2, dp_n * cpad, SUB), f32),
                vm((tok, 128), f32), vm((4, tok, 128), f32), vm((tp_n, tok, 128), f32), vm((8, 128), f32),
                vm((dp_n, 8, 128), f32), vm((dp_n, tok, 128), f32), vm((tp_n, tok, dim), f32),
                vm((dp_n, 8, 128), f32), vm((tp_n, rq, dim), f32), vm((tok, dim), bf16),
                dma((2,)), dma((SLOTS,)), dma, dma, dma((2,)), dma((2,)), dma((7,)), dma((7,)),
                dma((win // SUB,)), dma((win // SUB,)), dma((2,)), dma,
            ],
            compiler_params=pltpu.CompilerParams(collective_id=0, has_side_effects=True,
                                                 vmem_limit_bytes=66_000_000),
            name='head',
        )(hid_loc, norm_w.reshape(1, dim), mask_loc.astype(f32).reshape(tok, 1), emb_loc, teach_loc)
        return o_dw[7, 0], o_dh, o_emb[:cols, :vloc].T, o_dw.reshape(-1)[:dim]

    return jax.shard_map(device_fn, mesh=mesh, in_specs=(P('dp', None), P(None), P('tp', None), P('dp', 'tp'), P('dp')),
                         out_specs=(P(), P('dp', None), P('tp', 'dp'), P(None)), check_vma=False)
```

time: 1590 us -> 281 us (0.18)
  blocking collectives: 1270 us -> 0 us
  Pallas kernels: 0 us -> 265 us
  matrix products: 111 us -> 0 us
  local copies, waits for them, and re-layouts: 113 us -> 10 us
  waiting for transfers between devices: 39.6 us -> 0 us
  other arithmetic: 17.4 us -> 0.66 us
    unnamed x1 -> x0, blocking collectives: 860 us -> none
    psum x3 -> x0, blocking collectives: 405 us -> none  [the longest x1 331 us: device_fn(): loss_val = lax.psum(jnp.sum(weight * kl_tok), 'dp')]
    pallas_call x0 -> x1, Pallas kernels: none -> 265 us  [device_fn(): pl.pallas_call(functools.partial(body, (tp_n, dp_n, ny)), out_shape=(jax....]
    unnamed x14 -> x3, local copies, waits for them, and re-layouts: 113 us -> 0.65 us
    dot_general x3 -> x0, matrix products: 111 us -> none  [the longest x1 50.7 us: device_fn(): jnp.einsum('nv,nd->vd', d_raw, normed, preferred_element_type=jnp.float32)]
    psum x1 -> x0, waiting for transfers between devices: 39.6 us -> none  [device_fn(): lax.psum(jnp.dot(d_raw, emb_loc, preferred_element_type=jnp.float32), 'tp')]
  transfers between devices with their start and end apart: 5 -> 0, of which waited for: 1 -> 0; matrix products, arithmetic and copies ran while one was open for 2% -> 0% of each run, Pallas kernels for 0% -> 0%
where the time goes in v2:
time: 281 us; the launch traced here: 277 us
  Pallas kernels  265 us (94%)
  local copies, waits for them, and re-layouts  10 us (4%)
    pallas_call x1, Pallas kernels, device_fn(): pl.pallas_call(functools.partial(body, (tp_n, dp_n, ny)), out_shape=(jax....  265 us

profile of v2, /device:TPU:1, one launch (start us, length us, event | category | flops | bytes accessed | tf_op | source)
XLA Modules:
  0.0 276.7 jit_solution(1756107107111009342)
XLA Ops:
  0.6 0.7 convert_bitcast_fusion
  1.3 1.3 reshape.16.nw
  2.6 0.7 copy.9.mask
  3.3 265.4 %head.1 = (f32[32,38400]{1,0:T(8,128)}, bf16[64,896]{1,0:T(8,128)(2,1)}, f32[8,128]{1,0:T(8,128)}, f32[16,2,4,16,896]{4,3,2,1,0:T(8,128)}) custom-call(bf16[64,896]{1,0:T(8,128)(2,1)} %hid.1, bf16[1,896]{1,0:T(2,128)(2,1)} %reshape.16.nw, f32[64,1]{1,0:T(8,128)} %copy.9.mask, bf16[37984,896]{1,0:T(8,128)(2,1)} %emb.1, bf16[64,37984]{1,0:T(8,128)(2,1)} %teach.1), custom_call_target="tpu_custom_call" | custom-call | tf_op jit(solution)/shard_map/head/pallas_call | solution.py:496
  268.6 0.0 copy-start
  268.7 1.2 slice.12
  269.9 1.3 slice_bitcast_fusion.1
  271.2 4.9 %slice_bitcast_fusion = f32[37984,28]{0,1:T(8,128)} fusion(f32[32,38400]{1,0:T(8,128)} %get-tuple-element.9), kind=kLoop, calls=%fused_computation | loop fusion | bytes 8508416 | tf_op jit(solution)/shard_map/transpose | solution.py:518
  276.1 0.0 copy-done
  276.1 0.6 copy.11
Async XLA Ops:
  268.6 7.4 %copy-start = (bf16[64,896]{1,0:T(8,128)(2,1)S(1)}, bf16[64,896]{1,0:T(8,128)(2,1)}, u32[]{:S(2)}) copy-start(bf16[64,896]{1,0:T(8,128)(2,1)} %get-tuple-element.15) | copy-start | bytes 344068

commit v3 on v2

--- a/solution.py
+++ b/solution.py
@@ -18,8 +18,8 @@
 
 def body(cfg, hid, nw, mask, emb, teach, o_emb, o_dh, o_dw, gbuf,
          t_stage, th_buf, t_recv, tb, e_slot, e_sub, g_all, g_t, gin, dr_loc, r_blk, dr_blk, de_st,
-         m_buf, acc, st_tp, st_t, st_dp, st_all, dg_tp, dw_dp, xs_buf, gl_buf,
-         tb_sem, es_sem, sub_sem, gl_sem, gin_sem, loc_sem, snd_s, rcv_s, t_snd, t_rcv, de_snd, de_rcv):
+         rl_t, rl_e, m_buf, acc, st_tp, st_t, st_dp, st_all, dg_tp, dw_dp, xs_buf, gl_buf,
+         tb_sem, es_sem, sub_sem, gl_sem, gin_sem, loc_sem, snd_s, rcv_s, t_snd, t_rcv, de_snd, de_rcv, rt_rcv, rt_snd, re_rcv, re_snd):
     tp_n, dp_n, ny = cfg
     tok, dim = hid.shape
     vloc = emb.shape[0]
@@ -38,12 +38,44 @@
     chip = dp_i // 2
     core = dp_i % 2
 
+    def offset(k):
+        j = (k // 2 * 5) % chips
+        return j // ny, j % ny, k % 2
+
+    def device(dz, dy, dc):
+        return (((chip // ny + dz + nz) % nz) * ny + (chip % ny + dy + ny) % ny) * 2 + (core + dc) % 2
+
     def peer_chip(k):
-        j = (k * 5) % chips
-        return ((chip // ny + j // ny) % nz) * ny + (chip % ny + j % ny) % ny
+        dz, dy, _ = offset(2 * k)
+        return device(dz, dy, 0) // 2
 
     def peer(k):
-        return peer_chip(k // 2) * 2 + (core + k % 2) % 2
+        return device(*offset(k))
+
+    def is_two(v, n):
+        return (v // 2) * (1 - v % 2) if n == 4 else 0 * v
+
+    def far(k):
+        dz, dy, _ = offset(k)
+        return is_two(dz, nz) + is_two(dy, ny)
+
+    def hops(k):
+        dz, dy, dc = offset(k)
+        tz, ty = is_two(dz, nz), is_two(dy, ny)
+        slot = 2 * (tz * dy + (1 - tz) * (4 + (dz + 1) // 2)) + dc
+        rz, ry = (1 - 2 * dc) * tz, (1 - 2 * dc) * ty
+        return slot, (rz, ry), (dz - rz, dy - ry, dc)
+
+    def each_far(f):
+        if nz == 4 or ny == 4:
+            @pl.loop(1, dp_n)
+            def _(k):
+                pl.when(far(k) > 0)(functools.partial(f, k))
+
+    def each_near(f):
+        @pl.loop(1, dp_n)
+        def _(k):
+            pl.when(far(k) == 0)(functools.partial(f, k))
 
     def active(dev, s):
         return dev * win + s * SUB < vloc
@@ -153,19 +185,32 @@
     def _(k):
         ga_copy(peer_chip(k)).start()
 
-    def t_copy(dev, s):
+    def t_copy(dev, s, k):
         lane = pl.multiple_of(dev * win + s * SUB, SUB)
         return pltpu.make_async_remote_copy(t_stage.at[:, pl.ds(lane, SUB)], t_recv.at[dp_i, :, pl.ds(s * SUB, SUB)],
-                                            t_snd.at[s], t_rcv.at[s], device_id={'dp': dev}, device_id_type=MESH)
+                                            t_snd.at[k], t_rcv.at[s], device_id={'dp': dev}, device_id_type=MESH)
+
+    def t_first(k):
+        slot, (rz, ry), _ = hops(k)
+        dev = peer(k)
+        lane = pl.multiple_of(dev * win, SUB)
+
+        @pl.when(active(dev, 0))
+        def _():
+            pltpu.make_async_remote_copy(t_stage.at[:, pl.ds(lane, win)], rl_t.at[slot], t_snd.at[k], rt_rcv.at[slot],
+                                         device_id={'dp': device(rz, ry, 0)}, device_id_type=MESH).start()
+
+    each_far(t_first)
 
     for s in range(n_sub):
-        @pl.loop(1, dp_n)
-        def _(k, s=s):
+        def t_near(k, s=s):
             dev = peer(k)
 
             @pl.when(active(dev, s))
             def _():
-                t_copy(dev, s).start()
+                t_copy(dev, s, k).start()
+
+        each_near(t_near)
 
         @pl.when(active(dp_i, s))
         def _(s=s):
@@ -235,6 +280,30 @@
     @pl.loop(1, tp_n)
     def _(k):
         st_copy((tp_i + k) % tp_n).start()
+
+    def t_arrived(k):
+        slot, _, end = hops(k)
+
+        @pl.when(active(device(*end), 0))
+        def _():
+            pltpu.make_async_remote_copy(rl_t.at[slot], rl_t.at[slot], t_snd.at[0], rt_rcv.at[slot],
+                                         device_id={'dp': dp_i}, device_id_type=MESH).wait_recv()
+
+    each_far(t_arrived)
+
+    for s in range(n_sub):
+        def t_second(k, s=s):
+            slot, (rz, ry), end = hops(k)
+            dev = device(*end)
+            part = pl.ds(s * SUB, SUB)
+
+            @pl.when(active(dev, s))
+            def _():
+                pltpu.make_async_remote_copy(rl_t.at[slot, :, part], t_recv.at[device(-rz, -ry, 0), :, part],
+                                             rt_snd.at[slot], t_rcv.at[s], device_id={'dp': dev},
+                                             device_id_type=MESH).start()
+
+        each_far(t_second)
 
     sib = chip * 2 + (core + 1) % 2
     gb_wait = pltpu.make_async_remote_copy(gbuf.at[:, 0, pl.ds(0, tp_n - 1)], gbuf.at[:, 0, pl.ds(0, tp_n - 1)],
@@ -318,17 +387,17 @@
     gc_copy.wait()
 
     def gin_copy(d):
-        return pltpu.make_async_copy(gbuf.at[d // 2, d % 2], gin.at[d % 2], gin_sem.at[d % 2])
-
-    gin_copy(0).start()
-    gin_copy(1).start()
+        return pltpu.make_async_copy(gbuf.at[d // 2, d % 2], gin.at[d % 4], gin_sem.at[d % 4])
+
+    for d in range(min(4, dp_n)):
+        gin_copy(d).start()
 
     for d in range(dp_n):
         gin_copy(d).wait()
-        gv = (gin[d % 2].reshape(tok, dim) * scale)
+        gv = (gin[d % 4].reshape(tok, dim) * scale)
         g_all[pl.ds(d * tok, tok), :] = gv.astype(jnp.bfloat16)
-        if d + 2 < dp_n:
-            gin_copy(d + 2).start()
+        if d + 4 < dp_n:
+            gin_copy(d + 4).start()
 
     for d in range(0, dp_n, 2):
         gv = g_all[pl.ds(d * tok, 2 * tok), :].astype(jnp.float32).T
@@ -377,6 +446,27 @@
                                             o_emb.at[:, pl.ds(lane, SUB)], de_snd.at[s % 2], de_rcv,
                                             device_id={'dp': dev}, device_id_type=MESH)
 
+    def de_first(k, s):
+        slot, (rz, ry), _ = hops(k)
+        pltpu.make_async_remote_copy(de_st.at[s % 2, pl.ds(pl.multiple_of(peer(k) * cpad, 8), cpad)], rl_e.at[slot, s],
+                                     de_snd.at[s % 2], re_rcv.at[slot, s], device_id={'dp': device(rz, ry, 0)},
+                                     device_id_type=MESH).start()
+
+    def de_forward(s):
+        def go(k):
+            slot, (rz, ry), end = hops(k)
+            src = device(-rz, -ry, 0)
+
+            @pl.when(active(src, s))
+            def _():
+                lane = pl.multiple_of(src * win + s * SUB, SUB)
+                pltpu.make_async_remote_copy(rl_e.at[slot, s], rl_e.at[slot, s], de_snd.at[0], re_rcv.at[slot, s],
+                                             device_id={'dp': dp_i}, device_id_type=MESH).wait_recv()
+                pltpu.make_async_remote_copy(rl_e.at[slot, s], o_emb.at[:, pl.ds(lane, SUB)], re_snd.at[slot], de_rcv,
+                                             device_id={'dp': device(*end)}, device_id_type=MESH).start()
+
+        each_far(go)
+
     def de_local(s):
         lane = pl.multiple_of(dp_i * win + s * SUB, SUB)
         return pltpu.make_async_copy(de_st.at[s % 2, pl.ds(pl.multiple_of(dp_i * cpad, 8), cpad)],
@@ -397,7 +487,7 @@
         @pl.when(active(dp_i, s))
         def _(s=s):
             part = t_recv.at[pl.ds(0, dp_n - 1), :, pl.ds(s * SUB, SUB)]
-            pltpu.make_async_remote_copy(part, part, t_snd.at[s], t_rcv.at[s], device_id={'dp': dp_i},
+            pltpu.make_async_remote_copy(part, part, t_snd.at[0], t_rcv.at[s], device_id={'dp': dp_i},
                                          device_id_type=MESH).wait_recv()
 
             @pl.loop(0, dp_n // 4)
@@ -421,11 +511,15 @@
                 de_st[s % 2, rows, :] = lax.dot_general(g_t[rows, :], dr_blk[...], NN,
                                                         preferred_element_type=jnp.float32)
 
-            @pl.loop(1, dp_n)
-            def _(k):
-                de_copy(peer(k), s).start()
+            each_far(lambda k: de_first(k, s))
+            each_near(lambda k: de_copy(peer(k), s).start())
 
             de_local(s).start()
+
+        if s >= 1:
+            de_forward(s - 1)
+
+    de_forward(n_sub - 1)
 
     dw_wait = pltpu.make_async_remote_copy(dw_dp.at[pl.ds(0, dp_n - 1)], dw_dp.at[pl.ds(0, dp_n - 1)], snd_s.at[6],
                                            rcv_s.at[6], device_id={'dp': dp_i}, device_id_type=MESH)
@@ -440,24 +534,33 @@
     for w in (ga_wait, gb_wait, st_wait, sd_wait, dg_wait, dw_wait):
         w.wait_send()
 
-    def t_drain(s, n):
-        pltpu.make_async_remote_copy(t_stage.at[:, pl.ds(0, n * SUB)], t_stage.at[:, pl.ds(0, n * SUB)], t_snd.at[s],
-                                     t_rcv.at[s], device_id={'dp': dp_i}, device_id_type=MESH).wait_send()
-
-    for s in range(n_sub):
-        @pl.when(active(dp_i, s))
-        def _(s=s):
-            t_drain(s, n_act(s) - 1)
-
-        @pl.when(jnp.logical_not(active(dp_i, s)))
-        def _(s=s):
-            t_drain(s, n_act(s))
+    tail_n = -(-tail // SUB)
+
+    def drain(ref, sem):
+        pltpu.make_async_remote_copy(ref, ref, sem, t_rcv.at[0], device_id={'dp': dp_i}, device_id_type=MESH).wait_send()
+
+    def t_near_drain(k):
+        dev = peer(k)
+        pl.when(dev < last)(lambda: drain(t_stage.at[:, pl.ds(0, win)], t_snd.at[k]))
+        pl.when(dev == last)(lambda: drain(t_stage.at[:, pl.ds(0, tail_n * SUB)], t_snd.at[k]))
+
+    def far_drain(k):
+        slot, (rz, ry), end = hops(k)
+        dev = device(*end)
+        src = device(-rz, -ry, 0)
+        pl.when(peer(k) <= last)(lambda: drain(t_stage.at[:, pl.ds(0, win)], t_snd.at[k]))
+        pl.when(dev < last)(lambda: drain(rl_t.at[slot], rt_snd.at[slot]))
+        pl.when(dev == last)(lambda: drain(rl_t.at[slot, :, pl.ds(0, tail_n * SUB)], rt_snd.at[slot]))
+        pl.when(src < last)(lambda: drain(rl_e.at[slot], re_snd.at[slot]))
+        pl.when(src == last)(lambda: drain(rl_e.at[slot, pl.ds(0, tail_n)], re_snd.at[slot]))
+
+    each_near(t_near_drain)
+    each_far(far_drain)
 
     for s in range(max(0, n_sub - 2), n_sub):
         de_wait(s)
 
     total = sum(n_act(s) for s in range(n_sub))
-    tail_n = -(-tail // SUB)
 
     def de_drain(n):
         part = o_emb.at[:, pl.ds(0, n * SUB)]
@@ -493,6 +596,8 @@
         vm, dma = pltpu.VMEM, pltpu.SemaphoreType.DMA
         any_s, vm_s = pl.BlockSpec(memory_space=pl.ANY), pl.BlockSpec(memory_space=pltpu.VMEM)
         wide = n_ch * win
+        nz = dp_n // 2 // ny
+        n_rl = 2 * (nz * ny - (nz - (nz == 4)) * (ny - (ny == 4)))
         o_emb, o_dh, o_dw, _ = pl.pallas_call(
             functools.partial(body, (tp_n, dp_n, ny)),
             out_shape=(jax.ShapeDtypeStruct((cpad, wide), f32), jax.ShapeDtypeStruct((tok, dim), bf16),
@@ -503,16 +608,18 @@
             scratch_shapes=[
                 vm((tok, wide), f32), vm((tok, wide), f32), vm((dp_n, tok, win), f32), vm((2, 16, vloc), bf16),
                 vm((SLOTS, win, dim), bf16), vm((win, dim), bf16), vm((dp_n * tok, dim), bf16),
-                vm((dp_n * cpad, dp_n * tok), bf16), vm((2, tp_n, rq, dim), f32), vm((tok, win), bf16),
+                vm((dp_n * cpad, dp_n * tok), bf16), vm((4, tp_n, rq, dim), f32), vm((tok, win), bf16),
                 vm((4 * tok, SUB), f32), vm((dp_n * tok, SUB), bf16), vm((2, dp_n * cpad, SUB), f32),
+                vm((n_rl, tok, win), f32), vm((n_rl, win // SUB, cpad, SUB), f32),
                 vm((tok, 128), f32), vm((4, tok, 128), f32), vm((tp_n, tok, 128), f32), vm((8, 128), f32),
                 vm((dp_n, 8, 128), f32), vm((dp_n, tok, 128), f32), vm((tp_n, tok, dim), f32),
                 vm((dp_n, 8, 128), f32), vm((tp_n, rq, dim), f32), vm((tok, dim), bf16),
-                dma((2,)), dma((SLOTS,)), dma, dma, dma((2,)), dma((2,)), dma((7,)), dma((7,)),
-                dma((win // SUB,)), dma((win // SUB,)), dma((2,)), dma,
+                dma((2,)), dma((SLOTS,)), dma, dma, dma((4,)), dma((2,)), dma((7,)), dma((7,)),
+                dma((dp_n,)), dma((win // SUB,)), dma((2,)), dma,
+                dma((n_rl,)), dma((n_rl,)), dma((n_rl, win // SUB)), dma((n_rl,)),
             ],
             compiler_params=pltpu.CompilerParams(collective_id=0, has_side_effects=True,
-                                                 vmem_limit_bytes=66_000_000),
+                                                 vmem_limit_bytes=67_000_000),
             name='head',
         )(hid_loc, norm_w.reshape(1, dim), mask_loc.astype(f32).reshape(tok, 1), emb_loc, teach_loc)
         return o_dw[7, 0], o_dh, o_emb[:cols, :vloc].T, o_dw.reshape(-1)[:dim]

time: 281 us -> 261 us (0.929); the launches traced: 277 us -> 260 us
  Pallas kernels: 265 us -> 249 us
    pallas_call x1, Pallas kernels: 265 us -> 249 us  [device_fn(): pl.pallas_call(functools.partial(body, (tp_n, dp_n, ny)), out_shape=(jax....]
where the time goes in v3:
time: 261 us; the launch traced here: 260 us
  Pallas kernels  249 us (95%)
  local copies, waits for them, and re-layouts  10 us (4%)
    pallas_call x1, Pallas kernels, device_fn(): pl.pallas_call(functools.partial(body, (tp_n, dp_n, ny)), out_shape=(jax....  249 us

profile of v3, /device:TPU:1, one launch (start us, length us, event | category | flops | bytes accessed | tf_op | source)
XLA Modules:
  0.0 260.1 jit_solution(9364277718023117670)
XLA Ops:
  0.6 0.7 convert_bitcast_fusion
  1.3 1.3 reshape.16.nw
  2.6 0.7 copy.9.mask
  3.3 248.8 %head.1 = (f32[32,38400]{1,0:T(8,128)}, bf16[64,896]{1,0:T(8,128)(2,1)}, f32[8,128]{1,0:T(8,128)}, f32[16,2,4,16,896]{4,3,2,1,0:T(8,128)}) custom-call(bf16[64,896]{1,0:T(8,128)(2,1)} %hid.1, bf16[1,896]{1,0:T(2,128)(2,1)} %reshape.16.nw, f32[64,1]{1,0:T(8,128)} %copy.9.mask, bf16[37984,896]{1,0:T(8,128)(2,1)} %emb.1, bf16[64,37984]{1,0:T(8,128)(2,1)} %teach.1), custom_call_target="tpu_custom_call" | custom-call | tf_op jit(solution)/shard_map/head/pallas_call | solution.py:601
  252.1 0.0 copy-start
  252.1 1.2 slice.12
  253.3 1.3 slice_bitcast_fusion.1
  254.6 4.9 %slice_bitcast_fusion = f32[37984,28]{0,1:T(8,128)} fusion(f32[32,38400]{1,0:T(8,128)} %get-tuple-element.9), kind=kLoop, calls=%fused_computation | loop fusion | bytes 8508416 | tf_op jit(solution)/shard_map/transpose | solution.py:625
  259.5 0.0 copy-done
  259.5 0.6 copy.11
Async XLA Ops:
  252.1 7.4 %copy-start = (bf16[64,896]{1,0:T(8,128)(2,1)S(1)}, bf16[64,896]{1,0:T(8,128)(2,1)}, u32[]{:S(2)}) copy-start(bf16[64,896]{1,0:T(8,128)(2,1)} %get-tuple-element.15) | copy-start | bytes 344068

commit v4 on v2

v4 whole, which is shorter than its diff:
```python
import functools

import jax
import jax.numpy as jnp
from jax import lax
from jax.experimental import pallas as pl
from jax.experimental.pallas import tpu as pltpu
from jax.sharding import PartitionSpec as P

SOFT_CAP = 30.0
NORM_EPS = 1e-6
SUB = 256
ODD = (1, 3)
CORES = (0, 1)
SLOTS = 3
MESH = pl.DeviceIdType.MESH
NT = (((1,), (1,)), ((), ()))
NN = (((1,), (0,)), ((), ()))


def halves(j):
    return j // 2, j % 2


def way_of(d):
    return 1 - 2 * d


def m8(o, j):
    return o * 8 + j


def m2(o, dc):
    return o * 2 + dc


def body(cfg, hid, nw, mask, emb, teach, o_emb, o_dh, o_dw, gbuf, w1, r_a, r_b,
         t_stage, th_buf, t_recv, tb, e_slot, e_sub, g_all, g_t, gin, dr_loc, r_blk, dr_blk, de_st,
         e_1, e_a, e_b, mc_dp, m_buf, acc, st_tp, st_t, st_dp, st_all, dg_tp, dw_dp, xs_buf, gl_buf,
         tb_sem, es_sem, sub_sem, gl_sem, gin_sem, loc_sem, snd_s, rcv_s, t_rcv, de_snd, de_rcv, e1_rcv, ea_rcv, eb_rcv, e1_snd, e2_snd, eb_snd,
         w1_rcv, ra_rcv, rb_rcv, s1_snd, sa_snd, s2_snd, sb_snd):
    tp_n, dp_n, ny = cfg
    tok, dim = hid.shape
    vloc = emb.shape[0]
    win = t_recv.shape[2]
    n_sub = win // SUB
    n_ch = t_stage.shape[1] // win
    tail = vloc - (n_ch - 1) * win
    chips = dp_n // 2
    nz = chips // ny
    rq = tok // tp_n
    cpad = de_st.shape[1] // dp_n
    cols = dim // dp_n
    last = n_ch - 1
    tail_n = -(-tail // SUB)
    tp_i = lax.axis_index('tp')
    dp_i = lax.axis_index('dp')
    chip = dp_i // 2
    core = dp_i % 2

    zc, yc = chip // ny, chip % ny
    a_c, b_c = zc + core * (yc - zc), yc + core * (zc - yc)
    sa, sb = ny - core * (ny - 1), 1 + core * (ny - 1)

    def dev_ab(oa, ob, dc):
        return 2 * (((a_c + oa + 4) % 4) * sa + ((b_c + ob + 4) % 4) * sb) + (core + dc) % 2

    def dev_a(oa):
        return dev_ab(oa, 0, 0)

    def dev_b(ob):
        return dev_ab(0, ob, 0)

    def peer(k):
        j = (k // 2 * 5) % chips
        return ((zc + j // ny) % nz * ny + (yc + j % ny) % ny) * 2 + (core + k % 2) % 2

    def active(dev, s):
        return dev * win + s * SUB < vloc

    def n_act(s):
        return sum(1 for d in range(dp_n) if d * win + s * SUB < vloc)

    sib = chip * 2 + (core + 1) % 2

    def push(src, dst, snd, rcv, dev, axis='dp'):
        return pltpu.make_async_remote_copy(src, dst, snd, rcv, device_id={axis: dev}, device_id_type=MESH)

    def got(ref, sem):
        push(ref, ref, gl_sem, sem, dp_i).wait_recv()

    def sent(ref, sem):
        push(ref, ref, sem, gl_sem, dp_i).wait_send()

    def to_plane(buf, ch):
        @pl.loop(1, dp_n)
        def _(k):
            push(buf.at[dp_i], buf.at[dp_i], snd_s.at[ch], rcv_s.at[ch], peer(k)).start()

    def to_tp(ref, ch):
        @pl.loop(1, tp_n)
        def _(k):
            push(ref, ref, snd_s.at[ch], rcv_s.at[ch], (tp_i + k) % tp_n, 'tp').start()

    def others(buf):
        return buf.at[pl.ds(0, buf.shape[0] - 1)]

    barrier = pltpu.get_barrier_semaphore()

    @pl.loop(1, dp_n)
    def _(k):
        pl.semaphore_signal(barrier, inc=1, device_id={'dp': peer(k)}, device_id_type=MESH)

    @pl.loop(1, tp_n)
    def _(k):
        pl.semaphore_signal(barrier, inc=1, device_id={'tp': (tp_i + k) % tp_n}, device_id_type=MESH)

    def tb_copy(r):
        return pltpu.make_async_copy(teach.at[pl.ds(r * 16, 16)], tb.at[r % 2], tb_sem.at[r % 2])

    tb_copy(0).start()
    tb_copy(1).start()

    def e_copy(i, slot, rows):
        return pltpu.make_async_copy(emb.at[pl.ds(pl.multiple_of(i * win, 16), rows)],
                                     e_slot.at[slot, pl.ds(0, rows)], es_sem.at[slot])

    def e_start(i):
        @pl.when(i < last)
        def _():
            e_copy(i, i % SLOTS, win).start()

        @pl.when(i == last)
        def _():
            e_copy(i, i % SLOTS, tail).start()

    def e_wait(i):
        @pl.when(i < last)
        def _():
            e_copy(i, i % SLOTS, win).wait()

        @pl.when(i == last)
        def _():
            e_copy(i, i % SLOTS, tail).wait()

    def sub_copy(rows):
        return pltpu.make_async_copy(emb.at[pl.ds(pl.multiple_of(dp_i * win, 16), rows)],
                                     e_sub.at[pl.ds(0, rows)], sub_sem)

    @pl.when(dp_i < last)
    def _():
        sub_copy(win).start()

    @pl.when(dp_i == last)
    def _():
        sub_copy(tail).start()

    x = hid[...].astype(jnp.float32)
    scale = 1.0 + nw[...].astype(jnp.float32)
    inv = lax.rsqrt(jnp.mean(x * x, axis=-1, keepdims=True) + NORM_EPS)
    xs = x * inv
    xs_buf[...] = xs.reshape(tp_n, rq, dim)
    gl_buf[...] = (xs * scale).astype(jnp.bfloat16)

    own_g = pltpu.make_async_copy(xs_buf.at[tp_i], gbuf.at[chip, core, tp_i], gl_sem)
    own_g.start()

    m_loc = mask[...]
    mc_dp[dp_i] = jnp.broadcast_to(jnp.sum(m_loc, axis=0, keepdims=True), (8, 128))
    pl.semaphore_wait(barrier, dp_n - 1 + tp_n - 1)

    @pl.loop(1, chips)
    def _(k):
        push(xs_buf.at[tp_i], gbuf.at[chip, core, tp_i], snd_s.at[0], rcv_s.at[0], peer(2 * k)).start()


    to_plane(mc_dp, 7)

    pieces = [(c0, min(1024, vloc - c0)) for c0 in range(0, vloc, 1024)]
    full_p = vloc // 1024

    t_stage[:, pl.ds(vloc // 128 * 128, n_ch * win - vloc // 128 * 128)] = jnp.zeros(
        (tok, n_ch * win - vloc // 128 * 128), jnp.float32)
    for r in range(tok // 16):
        tb_copy(r).wait()
        rows = pl.ds(r * 16, 16)

        def conv(c0, width, mx):
            v = tb[r % 2, :, pl.ds(c0, width)].astype(jnp.float32)
            t_stage[rows, pl.ds(c0, width)] = v
            return v

        def step(i, mx):
            v = conv(pl.multiple_of(i * 1024, 128), 1024, mx)
            for q in range(8):
                mx = jnp.maximum(mx, v[:, q * 128:(q + 1) * 128])
            return mx

        mx = lax.fori_loop(0, full_p, step, jnp.full((16, 128), -jnp.inf, jnp.float32))
        m1 = jnp.max(mx, axis=-1, keepdims=True)
        if full_p * 1024 < vloc:
            v = conv(full_p * 1024, vloc - full_p * 1024, None)
            m1 = jnp.maximum(m1, jnp.max(v, axis=-1, keepdims=True))
        m_buf[rows, :] = jnp.broadcast_to(m1, (16, 128))
        if r + 2 < tok // 16:
            tb_copy(r + 2).start()

    for i in range(SLOTS):
        e_start(i)

    def t_win(dev):
        return t_stage.at[:, pl.ds(pl.multiple_of(dev * win, SUB), win)]

    def two_first(j):
        dest = dev_ab(2, *halves(j))
        hop = dev_a(way_of(j // 4))
        pl.when(dest <= last)(lambda: push(t_win(dest), r_a.at[j], s1_snd.at[16 + j], ra_rcv.at[j], hop).start())

    def one_first(o, j):
        dest = dev_ab(o, *halves(j))

        @pl.when(dest <= last)
        def _():
            pl.when(j < 2)(lambda: push(t_win(dest), t_recv.at[dp_i], s1_snd.at[m8(o, j)], t_rcv, dest).start())
            pl.when(j >= 2)(lambda: push(t_win(dest), w1.at[o, j], s1_snd.at[m8(o, j)], w1_rcv.at[m8(o, j)],
                                         dev_a(o)).start())

    def two_second(j):
        sign = way_of(j // 4)
        dest = dev_ab(sign, *halves(j))

        @pl.when(dest <= last)
        def _():
            got(r_a.at[j], ra_rcv.at[j])
            pl.when(j < 2)(lambda: push(r_a.at[j], t_recv.at[dev_a(-sign)], sa_snd.at[j], t_rcv, dest).start())
            pl.when(j >= 2)(lambda: push(r_a.at[j], w1.at[2, j], sa_snd.at[j], w1_rcv.at[16 + j],
                                         dev_a(sign)).start())

    def across(o, j):
        db, dc = halves(j)
        dest = dev_ab(0, db, dc)

        @pl.when(dest <= last)
        def _():
            if o == 0:
                src = t_win(dest)
            else:
                src = w1.at[o, j]
                got(src, w1_rcv.at[m8(o, j)])
            pl.when(db != 2)(lambda: push(src, t_recv.at[dev_a(-o)], s2_snd.at[m8(o, j)], t_rcv, dest).start())
            pl.when(db == 2)(lambda: push(src, r_b.at[m2(o, dc)], s2_snd.at[m8(o, j)], rb_rcv.at[m2(o, dc)],
                                          dev_b(way_of(dc))).start())

    def across_second(o, dc):
        sign = way_of(dc)
        dest = dev_ab(0, sign, dc)

        @pl.when(dest <= last)
        def _():
            got(r_b.at[m2(o, dc)], rb_rcv.at[m2(o, dc)])
            push(r_b.at[m2(o, dc)], t_recv.at[dev_ab(-o, -sign, 0)], sb_snd.at[m2(o, dc)], t_rcv, dest).start()

    @pl.loop(0, 4)
    def _(j):
        two_first(j)
        two_first(j + 4)

    @pl.loop(0, 8)
    def _(j):
        one_first(1, j)
        one_first(3, j)

    pl.when(sib <= last)(lambda: push(t_win(sib), t_recv.at[dp_i], s1_snd.at[1], t_rcv, sib).start())

    @pl.when(dp_i <= last)
    def _():
        t_recv[dp_i] = t_stage[:, pl.ds(pl.multiple_of(dp_i * win, SUB), win)]

    acc[...] = jnp.zeros_like(acc)
    lanes = lax.broadcasted_iota(jnp.int32, (tok, 128), 1)

    @pl.loop(0, n_ch)
    def _(i):
        e_wait(i)
        base = pl.multiple_of(i * win, SUB)
        th_buf[:, pl.ds(base, win)] = lax.dot_general(gl_buf[...], e_slot[i % SLOTS], NT,
                                                      preferred_element_type=jnp.float32)

        @pl.when(i + SLOTS < n_ch)
        def _():
            e_start(i + SLOTS)

        m_l = m_buf[...]
        a_s, a_1, a_2, a_x = acc[0], acc[1], acc[2], acc[3]
        for q in range(win // 128):
            at = pl.ds(pl.multiple_of(base + q * 128, 128), 128)
            th = jnp.tanh(th_buf[:, at] * (1.0 / SOFT_CAP))
            th_buf[:, at] = th
            z = SOFT_CAP * th
            ok = base + q * 128 + lanes < vloc
            e_s = jnp.where(ok, jnp.exp(z), 0.0)
            sh = t_stage[:, at] - m_l
            e_t = jnp.where(ok, jnp.exp(sh), 0.0)
            sh = jnp.where(ok, sh, 0.0)
            a_s = a_s + e_s
            a_1 = a_1 + e_t
            a_2 = a_2 + e_t * sh
            a_x = a_x + e_t * jnp.where(ok, z, 0.0)
        acc[0] = a_s
        acc[1] = a_1
        acc[2] = a_2
        acc[3] = a_x

    for i in range(SLOTS):
        e_start(i)

    parts = [m_buf[:, 0:1]] + [jnp.sum(acc[j], axis=-1, keepdims=True) for j in (1, 2, 3, 0)]
    tile = jnp.zeros((tok, 128), jnp.float32)
    for j, v in enumerate(parts):
        tile = jnp.where(lanes == j, v, tile)
    st_tp[tp_i] = tile

    to_tp(st_tp.at[tp_i], 2)
    got(others(st_tp), rcv_s.at[2])
    t_max = st_tp[0][:, 0:1]
    for q in range(1, tp_n):
        t_max = jnp.maximum(t_max, st_tp[q][:, 0:1])
    s_1 = s_2 = s_x = s_s = jnp.zeros((tok, 1), jnp.float32)
    for q in range(tp_n):
        v = st_tp[q]
        shift = v[:, 0:1] - t_max
        fac = jnp.exp(shift)
        s_1 = s_1 + fac * v[:, 1:2]
        s_2 = s_2 + fac * (v[:, 2:3] + shift * v[:, 1:2])
        s_x = s_x + fac * v[:, 3:4]
        s_s = s_s + v[:, 4:5]
    log_1 = jnp.log(s_1)
    kl = (s_2 - s_x) / s_1 - log_1 + jnp.log(s_s)
    lse_t = t_max + log_1
    inv_s = 1.0 / s_s
    tile = jnp.where(lanes == 0, lse_t, jnp.where(lanes == 1, inv_s, jnp.where(lanes == 2, m_loc, 0.0)))
    tile = jnp.concatenate([tile, jnp.zeros((128 - tok, 128), jnp.float32)], axis=0).T
    st_dp[dp_i] = tile[0:8]

    to_plane(st_dp, 4)

    own_g.wait()
    a_part = gbuf.at[pl.ds(0, chips - 1), 0, 0]
    got(a_part, rcv_s.at[0])
    to_tp(gbuf.at[:, core, tp_i], 1)

    @pl.loop(0, 8)
    def _(j):
        two_second(j)

    @pl.loop(2, 8)
    def _(j):
        across(0, j)

    got(others(mc_dp), rcv_s.at[7])
    m_cnt = jnp.sum(mc_dp[...], axis=0)[0:1, 0:1]
    w_loc = m_loc / m_cnt

    dg_tp[tp_i] = jnp.zeros((tok, dim), jnp.float32)

    @pl.loop(0, n_ch)
    def _(i):
        e_wait(i)
        base = pl.multiple_of(i * win, SUB)
        for q in range(win // 128):
            at = pl.ds(pl.multiple_of(base + q * 128, 128), 128)
            th = th_buf[:, at]
            p_s = jnp.exp(SOFT_CAP * th) * inv_s
            p_t = jnp.exp(t_stage[:, at] - lse_t)
            d = (p_s - p_t) * w_loc * (1.0 - th * th)
            ok = base + q * 128 + lanes < vloc
            dr_loc[:, pl.ds(q * 128, 128)] = jnp.where(ok, d, 0.0).astype(jnp.bfloat16)
        dg_tp[tp_i] += lax.dot_general(dr_loc[...], e_slot[i % SLOTS], NN, preferred_element_type=jnp.float32)

        @pl.when(i + SLOTS < n_ch)
        def _():
            e_start(i + SLOTS)

    to_tp(dg_tp.at[tp_i], 5)

    for o in ODD:
        @pl.loop(2, 8)
        def _(j, o=o):
            across(o, j)

    b_part = gbuf.at[:, 0, pl.ds(0, tp_n - 1)]
    got(b_part, rcv_s.at[1])
    gc_copy = push(gbuf.at[:, core], gbuf.at[:, core], snd_s.at[3], rcv_s.at[3], sib)
    gc_copy.start()

    for o in (2,):
        @pl.loop(2, 8)
        def _(j, o=o):
            across(o, j)

    gc_copy.wait()

    def gin_copy(d):
        return pltpu.make_async_copy(gbuf.at[d // 2, d % 2], gin.at[d % 4], gin_sem.at[d % 4])

    for d in range(min(4, dp_n)):
        gin_copy(d).start()

    for d in range(dp_n):
        gin_copy(d).wait()
        gv = (gin[d % 4].reshape(tok, dim) * scale)
        g_all[pl.ds(d * tok, tok), :] = gv.astype(jnp.bfloat16)
        if d + 4 < dp_n:
            gin_copy(d + 4).start()

    for d in range(0, dp_n, 2):
        gv = g_all[pl.ds(d * tok, 2 * tok), :].astype(jnp.float32).T
        for c in range(dp_n):
            gc = gv[c * cols:(c + 1) * cols]
            if cpad != cols:
                gc = jnp.concatenate([gc, jnp.zeros((cpad - cols, 2 * tok), jnp.float32)], axis=0)
            g_t[pl.ds(c * cpad, cpad), pl.ds(d * tok, 2 * tok)] = gc.astype(jnp.bfloat16)

    got(others(dg_tp), rcv_s.at[5])
    dg = dg_tp[0]
    for q in range(1, tp_n):
        dg = dg + dg_tp[q]
    x = hid[...].astype(jnp.float32)
    inv = lax.rsqrt(jnp.mean(x * x, axis=-1, keepdims=True) + NORM_EPS)
    dxs = dg * scale
    o_dh[...] = (inv * dxs - x * (inv * inv * inv * (jnp.sum(dxs * x, axis=-1, keepdims=True) / dim))).astype(jnp.bfloat16)
    dw = jnp.sum(dg * (x * inv), axis=0, keepdims=True)
    dw_dp[dp_i] = jnp.broadcast_to(jnp.sum(w_loc * kl, axis=0, keepdims=True), (8, 128))
    for j in range(dim // 128):
        dw_dp[dp_i, pl.ds(j, 1), :] = dw[:, j * 128:(j + 1) * 128]

    to_plane(dw_dp, 6)

    got(others(st_dp), rcv_s.at[4])

    @pl.loop(0, dp_n)
    def _(d):
        v = jnp.concatenate([st_dp[d], jnp.zeros((120, 128), jnp.float32)], axis=0).T
        st_all[d] = v[0:tok]

    for o in (0, 1, 3, 2):
        for dc in CORES:
            across_second(o, dc)

    @pl.when(dp_i < last)
    def _():
        sub_copy(win).wait()

    @pl.when(dp_i == last)
    def _():
        sub_copy(tail).wait()

    row_n = 4 * tok

    def de_src(dev, s):
        return de_st.at[s % 2, pl.ds(pl.multiple_of(dev * cpad, 8), cpad)]

    def de_dst(origin, s):
        return o_emb.at[:, pl.ds(pl.multiple_of(origin * win + s * SUB, SUB), SUB)]

    def de_local(s):
        return pltpu.make_async_copy(de_src(dp_i, s), de_dst(dp_i, s), loc_sem.at[s % 2])

    def de_first(s):
        snd = de_snd.at[s % 2]

        @pl.loop(0, 4)
        def _(j):
            for way in CORES:
                dest = dev_ab(2, *halves(j + 4 * way))
                push(de_src(dest, s), e_a.at[way, s, j], snd, ea_rcv.at[way, s], dev_a(way_of(way))).start()

        @pl.loop(0, 8)
        def _(j):
            for o in ODD:
                dest = dev_ab(o, *halves(j))
                src = de_src(dest, s)
                pl.when(j < 2)(lambda: push(src, de_dst(dp_i, s), snd, de_rcv, dest).start())
                pl.when(j >= 2)(lambda: push(src, e_1.at[o, s, j - 2], snd, e1_rcv.at[o, s], dev_a(o)).start())

        push(de_src(sib, s), de_dst(dp_i, s), snd, de_rcv, sib).start()
        de_turn(0, s, snd)
        de_local(s).start()

    def de_turn(o, s, snd):
        @pl.loop(2, 8)
        def _(j):
            db, dc = halves(j)
            dest = dev_ab(0, db, dc)
            src = e_1.at[o, s, j - 2] if o else de_src(dest, s)
            pl.when(db != 2)(lambda: push(src, de_dst(dev_a(-o), s), snd, de_rcv, dest).start())
            pl.when(db == 2)(lambda: push(src, e_b.at[o, dc, s], snd, eb_rcv.at[o, dc, s],
                                          dev_b(way_of(dc))).start())

    def de_two(s):
        for way in CORES:
            sign = way_of(way)
            origin = dev_a(-sign)

            @pl.when(active(origin, s))
            def _():
                got(e_a.at[way, s], ea_rcv.at[way, s])

                @pl.loop(0, 4)
                def _(j):
                    jj = j + 4 * way
                    dest = dev_ab(sign, *halves(jj))
                    src, snd = e_a.at[way, s, j], e2_snd.at[way]
                    pl.when(jj < 2)(lambda: push(src, de_dst(origin, s), snd, de_rcv, dest).start())
                    pl.when(jj >= 2)(lambda: push(src, e_1.at[2, s, jj - 2], snd, e1_rcv.at[2, s],
                                                  dev_a(sign)).start())

    def de_across(o, s):
        @pl.when(active(dev_a(-o), s))
        def _():
            got(e_1.at[o, s], e1_rcv.at[o, s])
            de_turn(o, s, e1_snd.at[o])

    def de_last(o, s):
        for dc in CORES:
            sign = way_of(dc)
            origin = dev_ab(-o, -sign, 0)

            @pl.when(active(origin, s))
            def _():
                src = e_b.at[o, dc, s]
                got(src, eb_rcv.at[o, dc, s])
                push(src, de_dst(origin, s), eb_snd.at[o, dc], de_rcv, dev_ab(0, sign, dc)).start()

    def de_step(k):
        def run(f, s, *o):
            if 0 <= s < n_sub:
                f(*o, s)

        run(de_two, k - 1)
        run(de_across, k - 1, 1)
        run(de_across, k - 1, 3)
        run(de_across, k - 2, 2)
        for o in (0, 1, 3):
            run(de_last, k - 2, o)
        run(de_last, k - 3, 2)

    def de_wait(s):
        @pl.when(active(dp_i, s))
        def _():
            sent(de_st.at[s % 2, pl.ds(0, (dp_n - 1) * cpad)], de_snd.at[s % 2])
            de_local(s).wait()

    pl.when(dp_i <= last)(lambda: got(t_recv.at[pl.ds(0, dp_n - 1)], t_rcv))

    for s in range(n_sub):
        if s >= 2:
            de_wait(s - 2)

        @pl.when(active(dp_i, s))
        def _(s=s):
            @pl.loop(0, dp_n // 4)
            def _(b):
                rows = pl.ds(pl.multiple_of(b * row_n, row_n), row_n)
                r_blk[...] = lax.dot_general(g_all[rows, :], e_sub[pl.ds(s * SUB, SUB), :], NT,
                                             preferred_element_type=jnp.float32)
                for q in range(row_n // 32):
                    d = b * 4 + q * 32 // tok
                    off = q * 32 % tok
                    th = jnp.tanh(r_blk[pl.ds(q * 32, 32), :] * (1.0 / SOFT_CAP))
                    sv = st_all[d, pl.ds(off, 32), :]
                    p_s = jnp.exp(SOFT_CAP * th) * sv[:, 1:2]
                    p_t = jnp.exp(t_recv[d, pl.ds(off, 32), pl.ds(s * SUB, SUB)] - sv[:, 0:1])
                    dv = (p_s - p_t) * (sv[:, 2:3] / m_cnt) * (1.0 - th * th)
                    dr_blk[pl.ds(pl.multiple_of(b * row_n + q * 32, 32), 32), :] = dv.astype(jnp.bfloat16)

            @pl.loop(0, de_st.shape[1] // 256)
            def _(b):
                rows = pl.ds(pl.multiple_of(b * 256, 256), 256)
                de_st[s % 2, rows, :] = lax.dot_general(g_t[rows, :], dr_blk[...], NN,
                                                        preferred_element_type=jnp.float32)

            de_first(s)

        de_step(s)

    for s in range(n_sub, n_sub + 3):
        de_step(s)

    got(others(dw_dp), rcv_s.at[6])
    tot = dw_dp[0]
    for d in range(1, dp_n):
        tot = tot + dw_dp[d]
    o_dw[...] = tot

    sent(a_part, snd_s.at[0])
    sent(b_part, snd_s.at[1])
    for buf, ch in ((st_tp, 2), (st_dp, 4), (dg_tp, 5), (dw_dp, 6), (mc_dp, 7)):
        sent(others(buf), snd_s.at[ch])

    one = t_recv.at[0]

    @pl.loop(0, 8)
    def _(j):
        for o in (1, 2, 3):
            pl.when(dev_ab(o, *halves(j)) <= last)(lambda o=o: sent(one, s1_snd.at[m8(o, j)]))
        pl.when(dev_ab(way_of(j // 4), *halves(j)) <= last)(lambda: sent(one, sa_snd.at[j]))

    pl.when(sib <= last)(lambda: sent(one, s1_snd.at[1]))

    @pl.loop(2, 8)
    def _(j):
        for o in range(4):
            pl.when(dev_ab(0, *halves(j)) <= last)(lambda o=o: sent(one, s2_snd.at[m8(o, j)]))

    for o in range(4):
        for dc in CORES:
            pl.when(dev_ab(0, way_of(dc), dc) <= last)(lambda o=o, dc=dc: sent(one, sb_snd.at[m2(o, dc)]))

    def e_sent(origin, part, sem):
        pl.when(origin < last)(lambda: sent(part(n_sub), sem))
        pl.when(origin == last)(lambda: sent(part(tail_n), sem))

    for way in CORES:
        e_sent(dev_ab(2 * way - 1, 0, 0), lambda n, way=way: e_a.at[way, pl.ds(0, n)], e2_snd.at[way])
    for o in range(4):
        if o:
            e_sent(dev_a(-o), lambda n, o=o: e_1.at[o, pl.ds(0, n)], e1_snd.at[o])
        for dc in CORES:
            e_sent(dev_ab(-o, 2 * dc - 1, 0), lambda n, o=o, dc=dc: e_b.at[o, dc, pl.ds(0, n)], eb_snd.at[o, dc])

    for s in range(max(0, n_sub - 2), n_sub):
        de_wait(s)

    total = sum(n_act(s) for s in range(n_sub))

    def de_drain(n):
        got(o_emb.at[:, pl.ds(0, n * SUB)], de_rcv)

    @pl.when(dp_i < last)
    def _():
        de_drain(total - n_sub)

    @pl.when(dp_i == last)
    def _():
        de_drain(total - tail_n)

    @pl.when(dp_i > last)
    def _():
        de_drain(total)


def solution(mesh):
    tp_n, dp_n = mesh.shape['tp'], mesh.shape['dp']
    ny = 4 if dp_n >= 32 else 1

    def device_fn(hid_loc, norm_w, emb_loc, teach_loc, mask_loc):
        tok, dim = hid_loc.shape
        vloc = emb_loc.shape[0]
        win = -(-vloc // (dp_n * SUB)) * SUB
        n_ch = -(-vloc // win)
        cols = dim // dp_n
        cpad = -(-cols // 8) * 8
        rq = tok // tp_n
        f32, bf16 = jnp.float32, jnp.bfloat16
        vm, dma = pltpu.VMEM, pltpu.SemaphoreType.DMA
        any_s, vm_s = pl.BlockSpec(memory_space=pl.ANY), pl.BlockSpec(memory_space=pltpu.VMEM)
        wide = n_ch * win
        n_sub = win // SUB
        o_emb, o_dh, o_dw = pl.pallas_call(
            functools.partial(body, (tp_n, dp_n, ny)),
            out_shape=(jax.ShapeDtypeStruct((cpad, wide), f32), jax.ShapeDtypeStruct((tok, dim), bf16),
                       jax.ShapeDtypeStruct((8, 128), f32),
                       jax.ShapeDtypeStruct((dp_n // 2, 2, tp_n, rq, dim), f32),
                       jax.ShapeDtypeStruct((4, 8, tok, win), f32), jax.ShapeDtypeStruct((8, tok, win), f32),
                       jax.ShapeDtypeStruct((8, tok, win), f32)),
            in_specs=[vm_s, vm_s, vm_s, any_s, any_s],
            out_specs=(any_s, vm_s, vm_s, any_s, any_s, any_s, any_s),
            scratch_shapes=[
                vm((tok, wide), f32), vm((tok, wide), f32), vm((dp_n, tok, win), f32), vm((2, 16, vloc), bf16),
                vm((SLOTS, win, dim), bf16), vm((win, dim), bf16), vm((dp_n * tok, dim), bf16),
                vm((dp_n * cpad, dp_n * tok), bf16), vm((4, tp_n, rq, dim), f32), vm((tok, win), bf16),
                vm((4 * tok, SUB), f32), vm((dp_n * tok, SUB), bf16), vm((2, dp_n * cpad, SUB), f32),
                vm((4, n_sub, 6, cpad, SUB), f32),
                vm((2, n_sub, 4, cpad, SUB), f32), vm((4, 2, n_sub, cpad, SUB), f32), vm((dp_n, 8, 128), f32),
                vm((tok, 128), f32), vm((4, tok, 128), f32), vm((tp_n, tok, 128), f32), vm((8, 128), f32),
                vm((dp_n, 8, 128), f32), vm((dp_n, tok, 128), f32), vm((tp_n, tok, dim), f32),
                vm((dp_n, 8, 128), f32), vm((tp_n, rq, dim), f32), vm((tok, dim), bf16),
                dma((2,)), dma((SLOTS,)), dma, dma, dma((4,)), dma((2,)), dma((8,)), dma((8,)),
                dma, dma((2,)), dma, dma((4, n_sub)), dma((2, n_sub)), dma((4, 2, n_sub)), dma((4,)), dma((2,)),
                dma((4, 2)),
                dma((32,)), dma((8,)), dma((8,)), dma((32,)), dma((8,)), dma((32,)), dma((8,)),
            ],
            compiler_params=pltpu.CompilerParams(collective_id=0, has_side_effects=True,
                                                 vmem_limit_bytes=67_000_000),
            name='head',
        )(hid_loc, norm_w.reshape(1, dim), mask_loc.astype(f32).reshape(tok, 1), emb_loc, teach_loc)[:3]
        return o_dw[7, 0], o_dh, o_emb[:cols, :vloc].T, o_dw.reshape(-1)[:dim]

    return jax.shard_map(device_fn, mesh=mesh, in_specs=(P('dp', None), P(None), P('tp', None), P('dp', 'tp'), P('dp')),
                         out_specs=(P(), P('dp', None), P('tp', 'dp'), P(None)), check_vma=False)
```

time: 281 us -> 219 us (0.78); the launches traced: 277 us -> 219 us
  Pallas kernels: 265 us -> 207 us
    pallas_call x1, Pallas kernels: 265 us -> 207 us  [device_fn(): pl.pallas_call(functools.partial(body, (tp_n, dp_n, ny)), out_shape=(jax....]
where the time goes in v4:
time: 219 us
  Pallas kernels  207 us (95%)
  local copies, waits for them, and re-layouts  10 us (5%)
    pallas_call x1, Pallas kernels, device_fn(): pl.pallas_call(functools.partial(body, (tp_n, dp_n, ny)), out_shape=(jax....  207 us
    transpose x1, local copies, waits for them, and re-layouts, device_fn(): return (o_dw[7, 0], o_dh, o_emb[:cols, :vloc].T, o_dw.reshape(-1)[:dim])  4.92 us

profile of v4, /device:TPU:1, one launch (start us, length us, event | category | flops | bytes accessed | tf_op | source)
XLA Modules:
  0.0 218.5 jit_solution(16011331646187017839)
XLA Ops:
  0.6 0.7 convert_bitcast_fusion
  1.3 1.3 reshape.16.nw
  2.6 0.7 copy.9.mask
  3.3 207.2 %head.1 = (f32[32,38400]{1,0:T(8,128)}, bf16[64,896]{1,0:T(8,128)(2,1)}, f32[8,128]{1,0:T(8,128)}, f32[16,2,4,16,896]{4,3,2,1,0:T(8,128)}, f32[4,8,64,1280]{3,2,...) custom-call(bf16[64,896]{1,0:T(8,128)(2,1)} %hid.1, bf16[1,896]{1,0:T(2,128)(2,1)} %reshape.16.nw, ...), custom_call_target="tpu_custom_call" | custom-call | tf_op jit(solution)/shard_map/head/pallas_call | solution.py:670
  210.5 0.0 copy-start
  210.5 1.2 slice.12
  211.7 1.3 slice_bitcast_fusion.1
  213.0 4.9 %slice_bitcast_fusion = f32[37984,28]{0,1:T(8,128)} fusion(f32[32,38400]{1,0:T(8,128)} %get-tuple-element.9), kind=kLoop, calls=%fused_computation | loop fusion | bytes 8508416 | tf_op jit(solution)/shard_map/transpose | solution.py:698
  217.9 0.0 copy-done
  217.9 0.6 copy.11
Async XLA Ops:
  210.5 7.4 %copy-start = (bf16[64,896]{1,0:T(8,128)(2,1)S(1)}, bf16[64,896]{1,0:T(8,128)(2,1)}, u32[]{:S(2)}) copy-start(bf16[64,896]{1,0:T(8,128)(2,1)} %get-tuple-element.15) | copy-start | bytes 344068

commit v5 on v4

--- a/solution.py
+++ b/solution.py
@@ -18,6 +18,10 @@
 NN = (((1,), (0,)), ((), ()))
 
 
+def col(v, j):
+    return v[:, j:j + 1]
+
+
 def halves(j):
     return j // 2, j % 2
 
@@ -37,7 +41,7 @@
 def body(cfg, hid, nw, mask, emb, teach, o_emb, o_dh, o_dw, gbuf, w1, r_a, r_b,
          t_stage, th_buf, t_recv, tb, e_slot, e_sub, g_all, g_t, gin, dr_loc, r_blk, dr_blk, de_st,
          e_1, e_a, e_b, mc_dp, m_buf, acc, st_tp, st_t, st_dp, st_all, dg_tp, dw_dp, xs_buf, gl_buf,
-         tb_sem, es_sem, sub_sem, gl_sem, gin_sem, loc_sem, snd_s, rcv_s, t_rcv, de_snd, de_rcv, e1_rcv, ea_rcv, eb_rcv, e1_snd, e2_snd, eb_snd,
+         tb_sem, es_sem, sub_sem, gl_sem, gin_sem, loc_sem, snd_s, rcv_s, t_rcv, de_snd, de_rcv, b_snd, b_rcv, e1_rcv, ea_rcv, eb_rcv, e1_snd, e2_snd, eb_snd,
          w1_rcv, ra_rcv, rb_rcv, s1_snd, sa_snd, s2_snd, sb_snd):
     tp_n, dp_n, ny = cfg
     tok, dim = hid.shape
@@ -260,6 +264,11 @@
             got(r_b.at[m2(o, dc)], rb_rcv.at[m2(o, dc)])
             push(r_b.at[m2(o, dc)], t_recv.at[dev_ab(-o, -sign, 0)], sb_snd.at[m2(o, dc)], t_rcv, dest).start()
 
+    def turn(o):
+        @pl.loop(2, 8)
+        def _(j):
+            across(o, j)
+
     @pl.loop(0, 4)
     def _(j):
         two_first(j)
@@ -276,11 +285,39 @@
     def _():
         t_recv[dp_i] = t_stage[:, pl.ds(pl.multiple_of(dp_i * win, SUB), win)]
 
+    a_part = gbuf.at[pl.ds(0, chips - 1), 0, 0]
+    up, down = (tp_i + 1) % tp_n, (tp_i + tp_n - 1) % tp_n
+    half = chips // 2
+
+    def rows_first():
+        own_g.wait()
+        got(a_part, rcv_s.at[0])
+        own = gbuf.at[:, core, tp_i]
+        push(own, own, b_snd.at[0], b_rcv.at[0], up, 'tp').start()
+        push(own, own, b_snd.at[1], b_rcv.at[1], down, 'tp').start()
+
+    def rows_second():
+        for way in CORES:
+            got(gbuf.at[:, 0, 0], b_rcv.at[way])
+        lo, hi = gbuf.at[pl.ds(0, half), core, down], gbuf.at[pl.ds(half, half), core, up]
+        push(lo, lo, b_snd.at[2], b_rcv.at[2], up, 'tp').start()
+        push(hi, hi, b_snd.at[3], b_rcv.at[3], down, 'tp').start()
+
+    b_half = gbuf.at[pl.ds(0, half), 0, 0]
+
+    def rows_sibling():
+        for way in CORES:
+            got(b_half, b_rcv.at[2 + way])
+        gc_copy.start()
+
+    gc_copy = push(gbuf.at[:, core], gbuf.at[:, core], snd_s.at[3], rcv_s.at[3], sib)
+
     acc[...] = jnp.zeros_like(acc)
     lanes = lax.broadcasted_iota(jnp.int32, (tok, 128), 1)
 
     @pl.loop(0, n_ch)
     def _(i):
+        pl.when(i == n_ch // 4)(rows_first)
         e_wait(i)
         base = pl.multiple_of(i * win, SUB)
         th_buf[:, pl.ds(base, win)] = lax.dot_general(gl_buf[...], e_slot[i % SLOTS], NT,
@@ -314,7 +351,7 @@
     for i in range(SLOTS):
         e_start(i)
 
-    parts = [m_buf[:, 0:1]] + [jnp.sum(acc[j], axis=-1, keepdims=True) for j in (1, 2, 3, 0)]
+    parts = [col(m_buf, 0)] + [jnp.sum(acc[j], axis=-1, keepdims=True) for j in (1, 2, 3, 0)]
     tile = jnp.zeros((tok, 128), jnp.float32)
     for j, v in enumerate(parts):
         tile = jnp.where(lanes == j, v, tile)
@@ -322,18 +359,18 @@
 
     to_tp(st_tp.at[tp_i], 2)
     got(others(st_tp), rcv_s.at[2])
-    t_max = st_tp[0][:, 0:1]
+    t_max = col(st_tp[0], 0)
     for q in range(1, tp_n):
-        t_max = jnp.maximum(t_max, st_tp[q][:, 0:1])
+        t_max = jnp.maximum(t_max, col(st_tp[q], 0))
     s_1 = s_2 = s_x = s_s = jnp.zeros((tok, 1), jnp.float32)
     for q in range(tp_n):
         v = st_tp[q]
-        shift = v[:, 0:1] - t_max
+        shift = col(v, 0) - t_max
         fac = jnp.exp(shift)
-        s_1 = s_1 + fac * v[:, 1:2]
-        s_2 = s_2 + fac * (v[:, 2:3] + shift * v[:, 1:2])
-        s_x = s_x + fac * v[:, 3:4]
-        s_s = s_s + v[:, 4:5]
+        s_1 = s_1 + fac * col(v, 1)
+        s_2 = s_2 + fac * (col(v, 2) + shift * col(v, 1))
+        s_x = s_x + fac * col(v, 3)
+        s_s = s_s + col(v, 4)
     log_1 = jnp.log(s_1)
     kl = (s_2 - s_x) / s_1 - log_1 + jnp.log(s_s)
     lse_t = t_max + log_1
@@ -344,18 +381,13 @@
 
     to_plane(st_dp, 4)
 
-    own_g.wait()
-    a_part = gbuf.at[pl.ds(0, chips - 1), 0, 0]
-    got(a_part, rcv_s.at[0])
-    to_tp(gbuf.at[:, core, tp_i], 1)
+    rows_second()
 
     @pl.loop(0, 8)
     def _(j):
         two_second(j)
 
-    @pl.loop(2, 8)
-    def _(j):
-        across(0, j)
+    turn(0)
 
     got(others(mc_dp), rcv_s.at[7])
     m_cnt = jnp.sum(mc_dp[...], axis=0)[0:1, 0:1]
@@ -365,6 +397,9 @@
 
     @pl.loop(0, n_ch)
     def _(i):
+        pl.when(i == n_ch // 3)(rows_sibling)
+        pl.when(i == n_ch // 2)(lambda: turn(1))
+        pl.when(i == n_ch * 2 // 3)(lambda: turn(3))
         e_wait(i)
         base = pl.multiple_of(i * win, SUB)
         for q in range(win // 128):
@@ -383,21 +418,6 @@
 
     to_tp(dg_tp.at[tp_i], 5)
 
-    for o in ODD:
-        @pl.loop(2, 8)
-        def _(j, o=o):
-            across(o, j)
-
-    b_part = gbuf.at[:, 0, pl.ds(0, tp_n - 1)]
-    got(b_part, rcv_s.at[1])
-    gc_copy = push(gbuf.at[:, core], gbuf.at[:, core], snd_s.at[3], rcv_s.at[3], sib)
-    gc_copy.start()
-
-    for o in (2,):
-        @pl.loop(2, 8)
-        def _(j, o=o):
-            across(o, j)
-
     gc_copy.wait()
 
     def gin_copy(d):
@@ -420,6 +440,8 @@
             if cpad != cols:
                 gc = jnp.concatenate([gc, jnp.zeros((cpad - cols, 2 * tok), jnp.float32)], axis=0)
             g_t[pl.ds(c * cpad, cpad), pl.ds(d * tok, 2 * tok)] = gc.astype(jnp.bfloat16)
+
+    turn(2)
 
     got(others(dg_tp), rcv_s.at[5])
     dg = dg_tp[0]
@@ -569,9 +591,9 @@
                     off = q * 32 % tok
                     th = jnp.tanh(r_blk[pl.ds(q * 32, 32), :] * (1.0 / SOFT_CAP))
                     sv = st_all[d, pl.ds(off, 32), :]
-                    p_s = jnp.exp(SOFT_CAP * th) * sv[:, 1:2]
-                    p_t = jnp.exp(t_recv[d, pl.ds(off, 32), pl.ds(s * SUB, SUB)] - sv[:, 0:1])
-                    dv = (p_s - p_t) * (sv[:, 2:3] / m_cnt) * (1.0 - th * th)
+                    p_s = jnp.exp(SOFT_CAP * th) * col(sv, 1)
+                    p_t = jnp.exp(t_recv[d, pl.ds(off, 32), pl.ds(s * SUB, SUB)] - col(sv, 0))
+                    dv = (p_s - p_t) * (col(sv, 2) / m_cnt) * (1.0 - th * th)
                     dr_blk[pl.ds(pl.multiple_of(b * row_n + q * 32, 32), 32), :] = dv.astype(jnp.bfloat16)
 
             @pl.loop(0, de_st.shape[1] // 256)
@@ -594,7 +616,9 @@
     o_dw[...] = tot
 
     sent(a_part, snd_s.at[0])
-    sent(b_part, snd_s.at[1])
+    for way in CORES:
+        sent(gbuf.at[:, 0, 0], b_snd.at[way])
+        sent(b_half, b_snd.at[2 + way])
     for buf, ch in ((st_tp, 2), (st_dp, 4), (dg_tp, 5), (dw_dp, 6), (mc_dp, 7)):
         sent(others(buf), snd_s.at[ch])
 
@@ -687,7 +711,7 @@
                 vm((dp_n, 8, 128), f32), vm((dp_n, tok, 128), f32), vm((tp_n, tok, dim), f32),
                 vm((dp_n, 8, 128), f32), vm((tp_n, rq, dim), f32), vm((tok, dim), bf16),
                 dma((2,)), dma((SLOTS,)), dma, dma, dma((4,)), dma((2,)), dma((8,)), dma((8,)),
-                dma, dma((2,)), dma, dma((4, n_sub)), dma((2, n_sub)), dma((4, 2, n_sub)), dma((4,)), dma((2,)),
+                dma, dma((2,)), dma, dma((4,)), dma((4,)), dma((4, n_sub)), dma((2, n_sub)), dma((4, 2, n_sub)), dma((4,)), dma((2,)),
                 dma((4, 2)),
                 dma((32,)), dma((8,)), dma((8,)), dma((32,)), dma((8,)), dma((32,)), dma((8,)),
             ],

time: 219 us -> 219 us (level)
  no operation moved by 1% of the time
where the time goes in v5:
time: 219 us
  Pallas kernels  207 us (95%)
  local copies, waits for them, and re-layouts  10 us (5%)
    pallas_call x1, Pallas kernels, device_fn(): pl.pallas_call(functools.partial(body, (tp_n, dp_n, ny)), out_shape=(jax....  207 us
    transpose x1, local copies, waits for them, and re-layouts, device_fn(): return (o_dw[7, 0], o_dh, o_emb[:cols, :vloc].T, o_dw.reshape(-1)[:dim])  4.92 us

profile of v5, /device:TPU:1, one launch (start us, length us, event | category | flops | bytes accessed | tf_op | source)
XLA Modules:
  0.0 218.7 jit_solution(17302997209590599666)
XLA Ops:
  0.6 0.7 convert_bitcast_fusion
  1.3 1.3 reshape.16.nw
  2.6 0.7 copy.9.mask
  3.3 207.4 %head.1 = (f32[32,38400]{1,0:T(8,128)}, bf16[64,896]{1,0:T(8,128)(2,1)}, f32[8,128]{1,0:T(8,128)}, f32[16,2,4,16,896]{4,3,2,1,0:T(8,128)}, f32[4,8,64,1280]{3,2,...) custom-call(bf16[64,896]{1,0:T(8,128)(2,1)} %hid.1, bf16[1,896]{1,0:T(2,128)(2,1)} %reshape.16.nw, ...), custom_call_target="tpu_custom_call" | custom-call | tf_op jit(solution)/shard_map/head/pallas_call | solution.py:694
  210.6 0.0 copy-start
  210.6 1.2 slice.12
  211.9 1.3 slice_bitcast_fusion.1
  213.1 4.9 %slice_bitcast_fusion = f32[37984,28]{0,1:T(8,128)} fusion(f32[32,38400]{1,0:T(8,128)} %get-tuple-element.9), kind=kLoop, calls=%fused_computation | loop fusion | bytes 8508416 | tf_op jit(solution)/shard_map/transpose | solution.py:722
  218.1 0.0 copy-done
  218.1 0.6 copy.11
Async XLA Ops:
  210.6 7.4 %copy-start = (bf16[64,896]{1,0:T(8,128)(2,1)S(1)}, bf16[64,896]{1,0:T(8,128)(2,1)}, u32[]{:S(2)}) copy-start(bf16[64,896]{1,0:T(8,128)(2,1)} %get-tuple-element.15) | copy-start | bytes 344068

commit v6 on v5

--- a/solution.py
+++ b/solution.py
@@ -10,6 +10,7 @@
 SOFT_CAP = 30.0
 NORM_EPS = 1e-6
 SUB = 256
+STRIP = 32
 ODD = (1, 3)
 CORES = (0, 1)
 SLOTS = 3
@@ -38,9 +39,9 @@
     return o * 2 + dc
 
 
-def body(cfg, hid, nw, mask, emb, teach, o_emb, o_dh, o_dw, gbuf, w1, r_a, r_b,
-         t_stage, th_buf, t_recv, tb, e_slot, e_sub, g_all, g_t, gin, dr_loc, r_blk, dr_blk, de_st,
-         e_1, e_a, e_b, mc_dp, m_buf, acc, st_tp, st_t, st_dp, st_all, dg_tp, dw_dp, xs_buf, gl_buf,
+def body(cfg, hid, nw, mask, emb, teach, o_emb, o_dh, o_dw, gbuf, e_1, e_a, e_b,
+         t_stage, th_buf, t_recv, tb, e_slot, g_all, g_t, gin, dr_loc, r_blk, dr_blk,
+         w1, r_a, r_b, mc_dp, m_buf, acc, st_tp, st_t, st_dp, st_all, dg_tp, dw_dp, xs_buf, gl_buf,
          tb_sem, es_sem, sub_sem, gl_sem, gin_sem, loc_sem, snd_s, rcv_s, t_rcv, de_snd, de_rcv, b_snd, b_rcv, e1_rcv, ea_rcv, eb_rcv, e1_snd, e2_snd, eb_snd,
          w1_rcv, ra_rcv, rb_rcv, s1_snd, sa_snd, s2_snd, sb_snd):
     tp_n, dp_n, ny = cfg
@@ -53,7 +54,7 @@
     chips = dp_n // 2
     nz = chips // ny
     rq = tok // tp_n
-    cpad = de_st.shape[1] // dp_n
+    cpad = o_emb.shape[0]
     cols = dim // dp_n
     last = n_ch - 1
     tail_n = -(-tail // SUB)
@@ -149,15 +150,7 @@
 
     def sub_copy(rows):
         return pltpu.make_async_copy(emb.at[pl.ds(pl.multiple_of(dp_i * win, 16), rows)],
-                                     e_sub.at[pl.ds(0, rows)], sub_sem)
-
-    @pl.when(dp_i < last)
-    def _():
-        sub_copy(win).start()
-
-    @pl.when(dp_i == last)
-    def _():
-        sub_copy(tail).start()
+                                     e_slot.at[0, pl.ds(0, rows)], sub_sem)
 
     x = hid[...].astype(jnp.float32)
     scale = 1.0 + nw[...].astype(jnp.float32)
@@ -213,7 +206,7 @@
         e_start(i)
 
     def t_win(dev):
-        return t_stage.at[:, pl.ds(pl.multiple_of(dev * win, SUB), win)]
+        return t_stage.at[:, pl.ds(pl.multiple_of(dev * win, 128), win)]
 
     def two_first(j):
         dest = dev_ab(2, *halves(j))
@@ -226,7 +219,7 @@
         @pl.when(dest <= last)
         def _():
             pl.when(j < 2)(lambda: push(t_win(dest), t_recv.at[dp_i], s1_snd.at[m8(o, j)], t_rcv, dest).start())
-            pl.when(j >= 2)(lambda: push(t_win(dest), w1.at[o, j], s1_snd.at[m8(o, j)], w1_rcv.at[m8(o, j)],
+            pl.when(j >= 2)(lambda: push(t_win(dest), w1.at[o - 1, j - 2], s1_snd.at[m8(o, j)], w1_rcv.at[m8(o, j)],
                                          dev_a(o)).start())
 
     def two_second(j):
@@ -237,7 +230,7 @@
         def _():
             got(r_a.at[j], ra_rcv.at[j])
             pl.when(j < 2)(lambda: push(r_a.at[j], t_recv.at[dev_a(-sign)], sa_snd.at[j], t_rcv, dest).start())
-            pl.when(j >= 2)(lambda: push(r_a.at[j], w1.at[2, j], sa_snd.at[j], w1_rcv.at[16 + j],
+            pl.when(j >= 2)(lambda: push(r_a.at[j], w1.at[1, j - 2], sa_snd.at[j], w1_rcv.at[16 + j],
                                          dev_a(sign)).start())
 
     def across(o, j):
@@ -249,7 +242,7 @@
             if o == 0:
                 src = t_win(dest)
             else:
-                src = w1.at[o, j]
+                src = w1.at[o - 1, j - 2]
                 got(src, w1_rcv.at[m8(o, j)])
             pl.when(db != 2)(lambda: push(src, t_recv.at[dev_a(-o)], s2_snd.at[m8(o, j)], t_rcv, dest).start())
             pl.when(db == 2)(lambda: push(src, r_b.at[m2(o, dc)], s2_snd.at[m8(o, j)], rb_rcv.at[m2(o, dc)],
@@ -269,6 +262,10 @@
         def _(j):
             across(o, j)
 
+    def turn_second(o):
+        for dc in CORES:
+            across_second(o, dc)
+
     @pl.loop(0, 4)
     def _(j):
         two_first(j)
@@ -283,7 +280,7 @@
 
     @pl.when(dp_i <= last)
     def _():
-        t_recv[dp_i] = t_stage[:, pl.ds(pl.multiple_of(dp_i * win, SUB), win)]
+        t_recv[dp_i] = t_stage[:, pl.ds(pl.multiple_of(dp_i * win, 128), win)]
 
     a_part = gbuf.at[pl.ds(0, chips - 1), 0, 0]
     up, down = (tp_i + 1) % tp_n, (tp_i + tp_n - 1) % tp_n
@@ -319,8 +316,9 @@
     def _(i):
         pl.when(i == n_ch // 4)(rows_first)
         e_wait(i)
-        base = pl.multiple_of(i * win, SUB)
-        th_buf[:, pl.ds(base, win)] = lax.dot_general(gl_buf[...], e_slot[i % SLOTS], NT,
+        base = pl.multiple_of(i * win, 128)
+        own = pl.ds(pl.multiple_of(i * tok, tok), tok)
+        th_buf[own, :] = lax.dot_general(gl_buf[...], e_slot[i % SLOTS], NT,
                                                       preferred_element_type=jnp.float32)
 
         @pl.when(i + SLOTS < n_ch)
@@ -331,8 +329,9 @@
         a_s, a_1, a_2, a_x = acc[0], acc[1], acc[2], acc[3]
         for q in range(win // 128):
             at = pl.ds(pl.multiple_of(base + q * 128, 128), 128)
-            th = jnp.tanh(th_buf[:, at] * (1.0 / SOFT_CAP))
-            th_buf[:, at] = th
+            part = pl.ds(q * 128, 128)
+            th = jnp.tanh(th_buf[own, part] * (1.0 / SOFT_CAP))
+            th_buf[own, part] = th
             z = SOFT_CAP * th
             ok = base + q * 128 + lanes < vloc
             e_s = jnp.where(ok, jnp.exp(z), 0.0)
@@ -401,22 +400,35 @@
         pl.when(i == n_ch // 2)(lambda: turn(1))
         pl.when(i == n_ch * 2 // 3)(lambda: turn(3))
         e_wait(i)
-        base = pl.multiple_of(i * win, SUB)
+        base = pl.multiple_of(i * win, 128)
+        own = pl.ds(pl.multiple_of(i * tok, tok), tok)
         for q in range(win // 128):
             at = pl.ds(pl.multiple_of(base + q * 128, 128), 128)
-            th = th_buf[:, at]
+            part = pl.ds(q * 128, 128)
+            th = th_buf[own, part]
             p_s = jnp.exp(SOFT_CAP * th) * inv_s
             p_t = jnp.exp(t_stage[:, at] - lse_t)
             d = (p_s - p_t) * w_loc * (1.0 - th * th)
             ok = base + q * 128 + lanes < vloc
-            dr_loc[:, pl.ds(q * 128, 128)] = jnp.where(ok, d, 0.0).astype(jnp.bfloat16)
+            dr_loc[:, part] = jnp.where(ok, d, 0.0).astype(jnp.bfloat16)
         dg_tp[tp_i] += lax.dot_general(dr_loc[...], e_slot[i % SLOTS], NN, preferred_element_type=jnp.float32)
 
         @pl.when(i + SLOTS < n_ch)
         def _():
             e_start(i + SLOTS)
 
+    @pl.when(dp_i < last)
+    def _():
+        sub_copy(win).start()
+
+    @pl.when(dp_i == last)
+    def _():
+        sub_copy(tail).start()
+
     to_tp(dg_tp.at[tp_i], 5)
+
+    turn(2)
+    turn_second(0)
 
     gc_copy.wait()
 
@@ -441,7 +453,8 @@
                 gc = jnp.concatenate([gc, jnp.zeros((cpad - cols, 2 * tok), jnp.float32)], axis=0)
             g_t[pl.ds(c * cpad, cpad), pl.ds(d * tok, 2 * tok)] = gc.astype(jnp.bfloat16)
 
-    turn(2)
+    for o in ODD:
+        turn_second(o)
 
     got(others(dg_tp), rcv_s.at[5])
     dg = dg_tp[0]
@@ -465,9 +478,7 @@
         v = jnp.concatenate([st_dp[d], jnp.zeros((120, 128), jnp.float32)], axis=0).T
         st_all[d] = v[0:tok]
 
-    for o in (0, 1, 3, 2):
-        for dc in CORES:
-            across_second(o, dc)
+    turn_second(2)
 
     @pl.when(dp_i < last)
     def _():
@@ -480,16 +491,16 @@
     row_n = 4 * tok
 
     def de_src(dev, s):
-        return de_st.at[s % 2, pl.ds(pl.multiple_of(dev * cpad, 8), cpad)]
+        return th_buf.at[pl.ds(pl.multiple_of(dev * cpad, 8), cpad), pl.ds(s * SUB, SUB)]
 
     def de_dst(origin, s):
-        return o_emb.at[:, pl.ds(pl.multiple_of(origin * win + s * SUB, SUB), SUB)]
+        return o_emb.at[:, pl.ds(pl.multiple_of(origin * win + s * SUB, 128), SUB)]
 
     def de_local(s):
-        return pltpu.make_async_copy(de_src(dp_i, s), de_dst(dp_i, s), loc_sem.at[s % 2])
+        return pltpu.make_async_copy(de_src(dp_i, s), de_dst(dp_i, s), loc_sem.at[s])
 
     def de_first(s):
-        snd = de_snd.at[s % 2]
+        snd = de_snd.at[s]
 
         @pl.loop(0, 4)
         def _(j):
@@ -570,36 +581,33 @@
     def de_wait(s):
         @pl.when(active(dp_i, s))
         def _():
-            sent(de_st.at[s % 2, pl.ds(0, (dp_n - 1) * cpad)], de_snd.at[s % 2])
+            sent(th_buf.at[pl.ds(0, (dp_n - 1) * cpad), pl.ds(0, SUB)], de_snd.at[s])
             de_local(s).wait()
 
     pl.when(dp_i <= last)(lambda: got(t_recv.at[pl.ds(0, dp_n - 1)], t_rcv))
 
     for s in range(n_sub):
-        if s >= 2:
-            de_wait(s - 2)
-
         @pl.when(active(dp_i, s))
         def _(s=s):
             @pl.loop(0, dp_n // 4)
             def _(b):
                 rows = pl.ds(pl.multiple_of(b * row_n, row_n), row_n)
-                r_blk[...] = lax.dot_general(g_all[rows, :], e_sub[pl.ds(s * SUB, SUB), :], NT,
+                r_blk[...] = lax.dot_general(g_all[rows, :], e_slot[0, pl.ds(s * SUB, SUB), :], NT,
                                              preferred_element_type=jnp.float32)
-                for q in range(row_n // 32):
-                    d = b * 4 + q * 32 // tok
-                    off = q * 32 % tok
-                    th = jnp.tanh(r_blk[pl.ds(q * 32, 32), :] * (1.0 / SOFT_CAP))
-                    sv = st_all[d, pl.ds(off, 32), :]
+                for q in range(row_n // STRIP):
+                    d = b * 4 + q * STRIP // tok
+                    off = q * STRIP % tok
+                    th = jnp.tanh(r_blk[pl.ds(q * STRIP, STRIP), :] * (1.0 / SOFT_CAP))
+                    sv = st_all[d, pl.ds(off, STRIP), :]
                     p_s = jnp.exp(SOFT_CAP * th) * col(sv, 1)
-                    p_t = jnp.exp(t_recv[d, pl.ds(off, 32), pl.ds(s * SUB, SUB)] - col(sv, 0))
+                    p_t = jnp.exp(t_recv[d, pl.ds(off, STRIP), pl.ds(s * SUB, SUB)] - col(sv, 0))
                     dv = (p_s - p_t) * (col(sv, 2) / m_cnt) * (1.0 - th * th)
-                    dr_blk[pl.ds(pl.multiple_of(b * row_n + q * 32, 32), 32), :] = dv.astype(jnp.bfloat16)
-
-            @pl.loop(0, de_st.shape[1] // 256)
+                    dr_blk[pl.ds(pl.multiple_of(b * row_n + q * STRIP, STRIP), STRIP), :] = dv.astype(jnp.bfloat16)
+
+            @pl.loop(0, dp_n * cpad // 256)
             def _(b):
                 rows = pl.ds(pl.multiple_of(b * 256, 256), 256)
-                de_st[s % 2, rows, :] = lax.dot_general(g_t[rows, :], dr_blk[...], NN,
+                th_buf[rows, pl.ds(s * SUB, SUB)] = lax.dot_general(g_t[rows, :], dr_blk[...], NN,
                                                         preferred_element_type=jnp.float32)
 
             de_first(s)
@@ -653,7 +661,7 @@
         for dc in CORES:
             e_sent(dev_ab(-o, 2 * dc - 1, 0), lambda n, o=o, dc=dc: e_b.at[o, dc, pl.ds(0, n)], eb_snd.at[o, dc])
 
-    for s in range(max(0, n_sub - 2), n_sub):
+    for s in range(n_sub):
         de_wait(s)
 
     total = sum(n_act(s) for s in range(n_sub))
@@ -681,7 +689,7 @@
     def device_fn(hid_loc, norm_w, emb_loc, teach_loc, mask_loc):
         tok, dim = hid_loc.shape
         vloc = emb_loc.shape[0]
-        win = -(-vloc // (dp_n * SUB)) * SUB
+        win = -(-vloc // (dp_n * 128)) * 128
         n_ch = -(-vloc // win)
         cols = dim // dp_n
         cpad = -(-cols // 8) * 8
@@ -696,22 +704,22 @@
             out_shape=(jax.ShapeDtypeStruct((cpad, wide), f32), jax.ShapeDtypeStruct((tok, dim), bf16),
                        jax.ShapeDtypeStruct((8, 128), f32),
                        jax.ShapeDtypeStruct((dp_n // 2, 2, tp_n, rq, dim), f32),
-                       jax.ShapeDtypeStruct((4, 8, tok, win), f32), jax.ShapeDtypeStruct((8, tok, win), f32),
-                       jax.ShapeDtypeStruct((8, tok, win), f32)),
+                       jax.ShapeDtypeStruct((4, n_sub, 6, cpad, SUB), f32),
+                       jax.ShapeDtypeStruct((2, n_sub, 4, cpad, SUB), f32),
+                       jax.ShapeDtypeStruct((4, 2, n_sub, cpad, SUB), f32)),
             in_specs=[vm_s, vm_s, vm_s, any_s, any_s],
             out_specs=(any_s, vm_s, vm_s, any_s, any_s, any_s, any_s),
             scratch_shapes=[
-                vm((tok, wide), f32), vm((tok, wide), f32), vm((dp_n, tok, win), f32), vm((2, 16, vloc), bf16),
-                vm((SLOTS, win, dim), bf16), vm((win, dim), bf16), vm((dp_n * tok, dim), bf16),
+                vm((tok, wide), f32), vm((n_ch * tok, win), f32), vm((dp_n, tok, win), f32), vm((2, 16, vloc), bf16),
+                vm((SLOTS, win, dim), bf16), vm((dp_n * tok, dim), bf16),
                 vm((dp_n * cpad, dp_n * tok), bf16), vm((4, tp_n, rq, dim), f32), vm((tok, win), bf16),
-                vm((4 * tok, SUB), f32), vm((dp_n * tok, SUB), bf16), vm((2, dp_n * cpad, SUB), f32),
-                vm((4, n_sub, 6, cpad, SUB), f32),
-                vm((2, n_sub, 4, cpad, SUB), f32), vm((4, 2, n_sub, cpad, SUB), f32), vm((dp_n, 8, 128), f32),
+                vm((4 * tok, SUB), f32), vm((dp_n * tok, SUB), bf16),
+                vm((3, 6, tok, win), f32), vm((8, tok, win), f32), vm((8, tok, win), f32), vm((dp_n, 8, 128), f32),
                 vm((tok, 128), f32), vm((4, tok, 128), f32), vm((tp_n, tok, 128), f32), vm((8, 128), f32),
                 vm((dp_n, 8, 128), f32), vm((dp_n, tok, 128), f32), vm((tp_n, tok, dim), f32),
                 vm((dp_n, 8, 128), f32), vm((tp_n, rq, dim), f32), vm((tok, dim), bf16),
-                dma((2,)), dma((SLOTS,)), dma, dma, dma((4,)), dma((2,)), dma((8,)), dma((8,)),
-                dma, dma((2,)), dma, dma((4,)), dma((4,)), dma((4, n_sub)), dma((2, n_sub)), dma((4, 2, n_sub)), dma((4,)), dma((2,)),
+                dma((2,)), dma((SLOTS,)), dma, dma, dma((4,)), dma((n_sub,)), dma((8,)), dma((8,)),
+                dma, dma((n_sub,)), dma, dma((4,)), dma((4,)), dma((4, n_sub)), dma((2, n_sub)), dma((4, 2, n_sub)), dma((4,)), dma((2,)),
                 dma((4, 2)),
                 dma((32,)), dma((8,)), dma((8,)), dma((32,)), dma((8,)), dma((32,)), dma((8,)),
             ],

time: 219 us -> 219 us (level)
  no operation moved by 1% of the time
where the time goes in v6:
time: 219 us; the launch traced here: 218 us
  Pallas kernels  207 us (95%)
  local copies, waits for them, and re-layouts  10 us (5%)
    pallas_call x1, Pallas kernels, device_fn(): pl.pallas_call(functools.partial(body, (tp_n, dp_n, ny)), out_shape=(jax....  207 us
    transpose x1, local copies, waits for them, and re-layouts, device_fn(): return (o_dw[7, 0], o_dh, o_emb[:cols, :vloc].T, o_dw.reshape(-1)[:dim])  4.96 us

profile of v6, /device:TPU:1, one launch (start us, length us, event | category | flops | bytes accessed | tf_op | source)
XLA Modules:
  0.0 218.3 jit_solution(336618525265197990)
XLA Ops:
  0.6 0.7 convert_bitcast_fusion
  1.3 1.3 reshape.16.nw
  2.6 0.7 copy.9.mask
  3.3 207.0 %head.1 = (f32[32,38400]{1,0:T(8,128)}, bf16[64,896]{1,0:T(8,128)(2,1)}, f32[8,128]{1,0:T(8,128)}, f32[16,2,4,16,896]{4,3,2,1,0:T(8,128)}, f32[4,5,6,32,256]{4,3...) custom-call(bf16[64,896]{1,0:T(8,128)(2,1)} %hid.1, bf16[1,896]{1,0:T(2,128)(2,1)} %reshape.16.nw, ...), custom_call_target="tpu_custom_call" | custom-call | tf_op jit(solution)/shard_map/head/pallas_call | solution.py:702
  210.3 1.2 slice.12
  211.4 1.3 slice_bitcast_fusion.1
  212.7 0.0 copy-start
  212.7 5.0 %slice_bitcast_fusion = f32[37984,28]{0,1:T(8,128)} fusion(f32[32,38400]{1,0:T(8,128)} %get-tuple-element.9), kind=kLoop, calls=%fused_computation | loop fusion | bytes 8508416 | tf_op jit(solution)/shard_map/transpose | solution.py:730
  217.7 0.0 copy-done
  217.7 0.6 copy.11
Async XLA Ops:
  212.7 5.0 %copy-start = (bf16[64,896]{1,0:T(8,128)(2,1)S(1)}, bf16[64,896]{1,0:T(8,128)(2,1)}, u32[]{:S(2)}) copy-start(bf16[64,896]{1,0:T(8,128)(2,1)} %get-tuple-element.15) | copy-start | bytes 344068

commit v7 on v6

--- a/solution.py
+++ b/solution.py
@@ -153,7 +153,7 @@
                                      e_slot.at[0, pl.ds(0, rows)], sub_sem)
 
     x = hid[...].astype(jnp.float32)
-    scale = 1.0 + nw[...].astype(jnp.float32)
+    scale = 1.0 + nw[...].astype(jnp.float32).reshape(1, dim)
     inv = lax.rsqrt(jnp.mean(x * x, axis=-1, keepdims=True) + NORM_EPS)
     xs = x * inv
     xs_buf[...] = xs.reshape(tp_n, rq, dim)
@@ -162,7 +162,9 @@
     own_g = pltpu.make_async_copy(xs_buf.at[tp_i], gbuf.at[chip, core, tp_i], gl_sem)
     own_g.start()
 
-    m_loc = mask[...]
+    diag = lax.broadcasted_iota(jnp.int32, (tok, tok), 0) == lax.broadcasted_iota(jnp.int32, (tok, tok), 1)
+    m_row = mask[...].astype(jnp.float32).reshape(1, tok)
+    m_loc = jnp.sum(jnp.where(diag, m_row, 0.0), axis=-1, keepdims=True)
     mc_dp[dp_i] = jnp.broadcast_to(jnp.sum(m_loc, axis=0, keepdims=True), (8, 128))
     pl.semaphore_wait(barrier, dp_n - 1 + tp_n - 1)
 
@@ -271,11 +273,6 @@
         two_first(j)
         two_first(j + 4)
 
-    @pl.loop(0, 8)
-    def _(j):
-        one_first(1, j)
-        one_first(3, j)
-
     pl.when(sib <= last)(lambda: push(t_win(sib), t_recv.at[dp_i], s1_snd.at[1], t_rcv, sib).start())
 
     @pl.when(dp_i <= last)
@@ -315,6 +312,12 @@
     @pl.loop(0, n_ch)
     def _(i):
         pl.when(i == n_ch // 4)(rows_first)
+
+        @pl.when(i % 3 + i // 24 * 3 == 0)
+        def _():
+            for o in ODD:
+                one_first(o, i // 3)
+
         e_wait(i)
         base = pl.multiple_of(i * win, 128)
         own = pl.ds(pl.multiple_of(i * tok, tok), tok)
@@ -726,7 +729,7 @@
             compiler_params=pltpu.CompilerParams(collective_id=0, has_side_effects=True,
                                                  vmem_limit_bytes=67_000_000),
             name='head',
-        )(hid_loc, norm_w.reshape(1, dim), mask_loc.astype(f32).reshape(tok, 1), emb_loc, teach_loc)[:3]
+        )(hid_loc, norm_w, mask_loc, emb_loc, teach_loc)[:3]
         return o_dw[7, 0], o_dh, o_emb[:cols, :vloc].T, o_dw.reshape(-1)[:dim]
 
     return jax.shard_map(device_fn, mesh=mesh, in_specs=(P('dp', None), P(None), P('tp', None), P('dp', 'tp'), P('dp')),

time: 219 us -> 217 us (level)
  no operation moved by 1% of the time
where the time goes in v7:
time: 217 us; the launch traced here: 216 us
  Pallas kernels  207 us (95%)
  local copies, waits for them, and re-layouts  8.07 us (4%)
    pallas_call x1, Pallas kernels, device_fn(): pl.pallas_call(functools.partial(body, (tp_n, dp_n, ny)), out_shape=(jax....  207 us
    transpose x1, local copies, waits for them, and re-layouts, device_fn(): return (o_dw[7, 0], o_dh, o_emb[:cols, :vloc].T, o_dw.reshape(-1)[:dim])  4.96 us

profile of v7, /device:TPU:1, one launch (start us, length us, event | category | flops | bytes accessed | tf_op | source)
XLA Modules:
  0.0 216.2 jit_solution(8692980621966009301)
XLA Ops:
  0.6 207.5 %head.1 = (f32[32,38400]{1,0:T(8,128)}, bf16[64,896]{1,0:T(8,128)(2,1)}, f32[8,128]{1,0:T(8,128)}, f32[16,2,4,16,896]{4,3,2,1,0:T(8,128)}, f32[4,5,6,32,256]{4,3...) custom-call(bf16[64,896]{1,0:T(8,128)(2,1)} %hid.1, bf16[896]{0:T(1024)(128)(2,1)} %nw.1, ...), custom_call_target="tpu_custom_call" | custom-call | tf_op jit(solution)/shard_map/head/pallas_call | solution.py:705
  208.1 1.2 slice.12
  209.3 1.3 slice_bitcast_fusion.1
  210.6 0.0 copy-start
  210.6 5.0 %slice_bitcast_fusion = f32[37984,28]{0,1:T(8,128)} fusion(f32[32,38400]{1,0:T(8,128)} %get-tuple-element.9), kind=kLoop, calls=%fused_computation | loop fusion | bytes 8508416 | tf_op jit(solution)/shard_map/transpose | solution.py:733
  215.6 0.0 copy-done
  215.6 0.6 copy.10
Async XLA Ops:
  210.6 5.0 %copy-start = (bf16[64,896]{1,0:T(8,128)(2,1)S(1)}, bf16[64,896]{1,0:T(8,128)(2,1)}, u32[]{:S(2)}) copy-start(bf16[64,896]{1,0:T(8,128)(2,1)} %get-tuple-element.15) | copy-start | bytes 344068

commit v8 on v7

--- a/solution.py
+++ b/solution.py
@@ -39,9 +39,9 @@
     return o * 2 + dc
 
 
-def body(cfg, hid, nw, mask, emb, teach, o_emb, o_dh, o_dw, gbuf, e_1, e_a, e_b,
+def body(cfg, hid, nw, mask, emb, teach, o_emb, o_dh, o_dw, gbuf, e_1, e_a,
          t_stage, th_buf, t_recv, tb, e_slot, g_all, g_t, gin, dr_loc, r_blk, dr_blk,
-         w1, r_a, r_b, mc_dp, m_buf, acc, st_tp, st_t, st_dp, st_all, dg_tp, dw_dp, xs_buf, gl_buf,
+         w1, r_a, r_b, e_b, mc_dp, m_buf, acc, st_tp, st_t, st_dp, st_all, dg_tp, dw_dp, xs_buf, gl_buf,
          tb_sem, es_sem, sub_sem, gl_sem, gin_sem, loc_sem, snd_s, rcv_s, t_rcv, de_snd, de_rcv, b_snd, b_rcv, e1_rcv, ea_rcv, eb_rcv, e1_snd, e2_snd, eb_snd,
          w1_rcv, ra_rcv, rb_rcv, s1_snd, sa_snd, s2_snd, sb_snd):
     tp_n, dp_n, ny = cfg
@@ -166,15 +166,6 @@
     m_row = mask[...].astype(jnp.float32).reshape(1, tok)
     m_loc = jnp.sum(jnp.where(diag, m_row, 0.0), axis=-1, keepdims=True)
     mc_dp[dp_i] = jnp.broadcast_to(jnp.sum(m_loc, axis=0, keepdims=True), (8, 128))
-    pl.semaphore_wait(barrier, dp_n - 1 + tp_n - 1)
-
-    @pl.loop(1, chips)
-    def _(k):
-        push(xs_buf.at[tp_i], gbuf.at[chip, core, tp_i], snd_s.at[0], rcv_s.at[0], peer(2 * k)).start()
-
-
-    to_plane(mc_dp, 7)
-
     pieces = [(c0, min(1024, vloc - c0)) for c0 in range(0, vloc, 1024)]
     full_p = vloc // 1024
 
@@ -206,6 +197,15 @@
 
     for i in range(SLOTS):
         e_start(i)
+
+    pl.semaphore_wait(barrier, dp_n - 1 + tp_n - 1)
+
+    @pl.loop(1, chips)
+    def _(k):
+        push(xs_buf.at[tp_i], gbuf.at[chip, core, tp_i], snd_s.at[0], rcv_s.at[0], peer(2 * k)).start()
+
+
+    to_plane(mc_dp, 7)
 
     def t_win(dev):
         return t_stage.at[:, pl.ds(pl.multiple_of(dev * win, 128), win)]
@@ -708,16 +708,16 @@
                        jax.ShapeDtypeStruct((8, 128), f32),
                        jax.ShapeDtypeStruct((dp_n // 2, 2, tp_n, rq, dim), f32),
                        jax.ShapeDtypeStruct((4, n_sub, 6, cpad, SUB), f32),
-                       jax.ShapeDtypeStruct((2, n_sub, 4, cpad, SUB), f32),
-                       jax.ShapeDtypeStruct((4, 2, n_sub, cpad, SUB), f32)),
+                       jax.ShapeDtypeStruct((2, n_sub, 4, cpad, SUB), f32)),
             in_specs=[vm_s, vm_s, vm_s, any_s, any_s],
-            out_specs=(any_s, vm_s, vm_s, any_s, any_s, any_s, any_s),
+            out_specs=(any_s, vm_s, vm_s, any_s, any_s, any_s),
             scratch_shapes=[
                 vm((tok, wide), f32), vm((n_ch * tok, win), f32), vm((dp_n, tok, win), f32), vm((2, 16, vloc), bf16),
                 vm((SLOTS, win, dim), bf16), vm((dp_n * tok, dim), bf16),
                 vm((dp_n * cpad, dp_n * tok), bf16), vm((4, tp_n, rq, dim), f32), vm((tok, win), bf16),
                 vm((4 * tok, SUB), f32), vm((dp_n * tok, SUB), bf16),
-                vm((3, 6, tok, win), f32), vm((8, tok, win), f32), vm((8, tok, win), f32), vm((dp_n, 8, 128), f32),
+                vm((3, 6, tok, win), f32), vm((8, tok, win), f32), vm((8, tok, win), f32),
+                vm((4, 2, n_sub, cpad, SUB), f32), vm((dp_n, 8, 128), f32),
                 vm((tok, 128), f32), vm((4, tok, 128), f32), vm((tp_n, tok, 128), f32), vm((8, 128), f32),
                 vm((dp_n, 8, 128), f32), vm((dp_n, tok, 128), f32), vm((tp_n, tok, dim), f32),
                 vm((dp_n, 8, 128), f32), vm((tp_n, rq, dim), f32), vm((tok, dim), bf16),

time: 217 us -> 218 us (level)
  no operation moved by 1% of the time
where the time goes in v8:
time: 218 us; the launch traced here: 217 us
  Pallas kernels  209 us (96%)
  local copies, waits for them, and re-layouts  8.06 us (4%)
    pallas_call x1, Pallas kernels, device_fn(): pl.pallas_call(functools.partial(body, (tp_n, dp_n, ny)), out_shape=(jax....  209 us
    transpose x1, local copies, waits for them, and re-layouts, device_fn(): return (o_dw[7, 0], o_dh, o_emb[:cols, :vloc].T, o_dw.reshape(-1)[:dim])  4.96 us

profile of v8, /device:TPU:1, one launch (start us, length us, event | category | flops | bytes accessed | tf_op | source)
XLA Modules:
  0.0 217.2 jit_solution(122116991313355224)
XLA Ops:
  0.6 208.5 %head.1 = (f32[32,38400]{1,0:T(8,128)}, bf16[64,896]{1,0:T(8,128)(2,1)}, f32[8,128]{1,0:T(8,128)}, f32[16,2,4,16,896]{4,3,2,1,0:T(8,128)}, f32[4,5,6,32,256]{4,3,2,1,0:T(8,128)}, /*index=5*/f32[2,5,4,32,256]{4,3,2,1,0:T(8,128)}) custom-call(bf16[64,896]{1,0:T(8,128)(2,1)} %hid.1, bf16[896]{0:T(1024)(128)(2,1)} %nw.1, s32[64]{0:T(128)} %mask.1, ...), custom_call_target="tpu_custom_call" | custom-call | tf_op jit(solution)/shard_map/head/pallas_call | solution.py:705
  209.2 1.2 slice.12
  210.3 1.3 slice_bitcast_fusion.1
  211.6 0.0 copy-start
  211.6 5.0 %slice_bitcast_fusion = f32[37984,28]{0,1:T(8,128)} fusion(f32[32,38400]{1,0:T(8,128)} %get-tuple-element.9), kind=kLoop, calls=%fused_computation | loop fusion | bytes 8508416 | tf_op jit(solution)/shard_map/transpose | solution.py:733
  216.6 0.0 copy-done
  216.6 0.6 copy.10
Async XLA Ops:
  211.6 5.0 %copy-start = (bf16[64,896]{1,0:T(8,128)(2,1)S(1)}, bf16[64,896]{1,0:T(8,128)(2,1)}, u32[]{:S(2)}) copy-start(bf16[64,896]{1,0:T(8,128)(2,1)} %get-tuple-element.15) | copy-start | bytes 344068
